TPU v7x, 32 devices: a whole 2x2x4 slice. The times are simulated.
32 devices in a mesh: seq: 8 (over z, x), head: 4 (over y, core).
Axes of the slice: x: 2, y: 2, z: 4, core: 2. Of those that a mesh axis runs over, the one named last changes fastest.
Arguments:
- queries: bfloat16 [1024, 3072], P('seq', 'head'), may hold values from -8 to 8
- latents: bfloat16 [1024, 576], P('seq'), may hold values from -8 to 8
- key_up: bfloat16 [512, 2048], P(None, 'head'), may hold values from -0.25 to 0.25
- value_up: bfloat16 [512, 2048], P(None, 'head'), may hold values from -0.25 to 0.25
- out_grad: bfloat16 [1024, 2048], P('seq', 'head'), may hold values from -48 to 48
- positions: int32 [1024], P('seq'), may hold values from 0 to 1023, as said below
Outputs:
- query_grad: bfloat16 [1024, 3072], P('seq', 'head')
- latent_grad: float32 [1024, 576], P('seq')
- key_up_grad: float32 [512, 2048], P(None, 'head')
- value_up_grad: float32 [512, 2048], P(None, 'head')
Inputs may be any that keep to these rules, and one draw needn't show every extreme that they name: Every position from 0 to 1023 occurs once; positions come in stripes of 128 consecutive positions in ascending order, each stripe whole within the rows of one device.
All inputs are finite; a program needn't handle non-finite values.
Results may differ from a plain program's by a relative error of at most 0.0084.
Values may be sent and summed in bfloat16 or wider, within the bound.
A program may use at most 64 MiB of HBM per device.

v0:
```python
import itertools
import math

import jax
import jax.numpy as jnp
from jax import lax
from jax.experimental import pallas as pl
from jax.experimental.pallas import tpu as pltpu
from jax.sharding import PartitionSpec as P

D_LAT = 512
D_ROPE = 64
D_NOPE = 128
D_V = 128
D_QK = D_NOPE + D_ROPE
LANE = 128
NEG = -1e30
MESH = pl.DeviceIdType.MESH
F32 = jnp.float32
BF16 = jnp.bfloat16


def bit(index, b):
    return (index // (1 << b)) % 2


def flip(index, b):
    return index + (1 << b) * (1 - 2 * bit(index, b))


def with_bits(index, bits, values):
    for b, value in zip(bits, values):
        index = index + (1 << b) * (value - bit(index, b))
    return index


def choices(bits):
    return list(itertools.product((0, 1), repeat=len(bits)))


def nn(a, b):
    return lax.dot_general(a, b, (((1,), (0,)), ((), ())), preferred_element_type=F32)


def nt(a, b):
    return lax.dot_general(a, b, (((1,), (1,)), ((), ())), preferred_element_type=F32)


def tn(a, b):
    return lax.dot_general(a, b, (((0,), (0,)), ((), ())), preferred_element_type=F32)


class Sems:
    def __init__(self, send, recv):
        self.send, self.recv, self.used = send, recv, 0
        self.sent = []

    def copy(self, src, dst, device):
        k = self.used
        self.used += 1
        copy = pltpu.make_async_remote_copy(
            src_ref=src,
            dst_ref=dst,
            send_sem=self.send.at[k],
            recv_sem=self.recv.at[k],
            device_id=device,
            device_id_type=MESH,
        )
        copy.start()
        self.sent.append(copy)
        return copy


def reduce_steps(sems, me, order, device_of, part, slots):
    slot = 0
    for k, b in enumerate(order):
        rest = order[k + 1 :]
        copies = []
        for values in choices(rest):
            leaving = with_bits(flip(me, b), rest, values)
            copies.append((sems.copy(part(leaving), slots(slot), device_of(flip(me, b))), slot, values))
            slot += 1
        yield
        for copy, at, values in copies:
            copy.wait_recv()
            kept = part(with_bits(me, rest, values))
            kept[...] = (kept[...].astype(F32) + slots(at)[...].astype(F32)).astype(BF16)


def gather_steps(sems, me, order, device_of, part):
    for k, b in enumerate(order):
        done = order[:k]
        copies = []
        for values in choices(done):
            held = with_bits(me, done, values)
            copies.append(sems.copy(part(held), part(held), device_of(flip(me, b))))
        yield
        for copy in copies:
            copy.wait_recv()


def kernel(
    nseq, nhead,
    q_ref, lat_ref, ku_ref, vu_ref, do_ref, pos_ref,
    dq_ref, dl_ref, dk_ref, dv_ref,
    lat, kk, vv, sc, dp, top, kv, rope, gk, gv, fk, fv, rk, rv, lb, rh, rl, fl, dqs,
    send, recv,
):
    seq, head = lax.axis_index("seq"), lax.axis_index("head")
    seq_bits = list(range(nseq.bit_length() - 1))
    head_bits = list(range(nhead.bit_length() - 1))
    rows = lat_ref.shape[0]
    half = rows // 2
    heads = ku_ref.shape[1] // D_NOPE
    qrows = q_ref.shape[0]
    scale = 1.0 / math.sqrt(D_QK)
    sems = Sems(send, recv)

    def on_seq(s):
        return (s, head)

    def on_head(h):
        return (seq, h)

    barrier = pltpu.get_barrier_semaphore()
    for b in seq_bits:
        pl.semaphore_signal(barrier, inc=1, device_id=on_seq(flip(seq, b)), device_id_type=MESH)
    for b in head_bits:
        pl.semaphore_signal(barrier, inc=1, device_id=on_head(flip(head, b)), device_id_type=MESH)
    pl.semaphore_wait(barrier, len(seq_bits) + len(head_bits))

    core = bit(head, 0)
    other = on_head(flip(head, 0))
    top[...] = jnp.full(top.shape, NEG, F32)

    def at_rows(part):
        return pl.ds(pl.multiple_of(part * rows, rows), rows)

    def take(part):
        here = at_rows(part)
        block = lat[here, :]
        comp = block[:, :D_LAT]
        keys = nn(comp, ku_ref[...]).astype(BF16)
        vals = nn(comp, vu_ref[...]).astype(BF16)
        kk[here, :] = keys
        vv[here, :] = vals
        kpos = block[:, D_LAT + D_ROPE :].astype(F32)
        kpos = kpos[:, 0:1] * float(LANE) + kpos[:, 1:2]
        visible = kpos <= pos_ref[...]
        rkeys = block[:, D_LAT : D_LAT + D_ROPE]
        for h in range(heads):
            qn = q_ref[:, h * D_QK : h * D_QK + D_NOPE]
            qr = q_ref[:, h * D_QK + D_NOPE : (h + 1) * D_QK]
            s = nt(keys[:, h * D_NOPE : (h + 1) * D_NOPE], qn) + nt(rkeys, qr)
            s = jnp.where(visible, s * scale, NEG)
            sc[h, here, :] = s
            top[h : h + 1, :] = jnp.maximum(top[h : h + 1, :], jnp.max(s, axis=0, keepdims=True))
            dp[h, here, :] = nt(vals[:, h * D_V : (h + 1) * D_V], do_ref[:, h * D_V : (h + 1) * D_V])

    piece = half // 2
    down = seq_bits[::-1]
    orders = [down, down[:-2] + down[-2:][::-1]]
    lat[at_rows(seq), :] = lat_ref[...]

    def piece_of(part, p):
        start = part * rows + core * half + p * piece
        return lat.at[pl.ds(pl.multiple_of(start, piece), piece)]

    def bring(p, order):
        own = lat_ref.at[pl.ds(pl.multiple_of(core * half + p * piece, piece), piece)]
        for k, b in enumerate(order):
            copies = []
            for values in choices(order[:k]):
                held = with_bits(seq, order[:k], values)
                src = own if k == 0 else piece_of(held, p)
                part = with_bits(flip(seq, b), order[:k], values)
                copies.append((sems.copy(src, piece_of(held, p), on_seq(flip(seq, b))), part))
            yield None
            passed = []
            for copy, part in copies:
                copy.wait_recv()
                passed.append(sems.copy(piece_of(part, p), piece_of(part, p), other))
            yield passed

    brings = [bring(p, order) for p, order in enumerate(orders)]
    for g in brings:
        next(g)
    common = max(len(down) - 2, 0)
    fresh, waiting = [seq], []
    for k in range(len(down)):
        passed = []
        for g in brings:
            passed += next(g)
            next(g, None)
        for part in fresh:
            take(part)
        fresh = []
        waiting += passed
        if k < common:
            for copy in waiting:
                copy.wait_recv()
            waiting = []
            fresh = [with_bits(flip(seq, down[k]), down[:k], values) for values in choices(down[:k])]
    for part in fresh:
        take(part)
    for copy in waiting:
        copy.wait_recv()
    tail = down[common:]
    for late in choices(tail):
        if not any(late):
            continue
        base = seq
        for b, turned in zip(tail, late):
            base = flip(base, b) if turned else base
        for values in choices(down[:common]):
            take(with_bits(base, down[:common], values))

    tile = math.gcd(lat.shape[0], 256)
    tiles = lat.shape[0] // tile

    def sums(t, carry):
        here = pl.ds(pl.multiple_of(t * tile, tile), tile)
        out = []
        for h in range(heads):
            total, weighted = carry[h]
            p = jnp.exp(sc[h, here, :] - top[h : h + 1, :])
            sc[h, here, :] = p
            total = total + jnp.sum(p, axis=0, keepdims=True)
            weighted = weighted + jnp.sum(p * dp[h, here, :], axis=0, keepdims=True)
            out.append((total, weighted))
        return tuple(out)

    zero = jnp.zeros((1, qrows), F32)
    stats = lax.fori_loop(0, tiles, sums, tuple((zero, zero) for _ in range(heads)))
    inv = [1.0 / total for total, _ in stats]
    delta = [weighted / total for total, weighted in stats]
    dqs[...] = jnp.zeros(dqs.shape, F32)

    def grads(t, carry):
        here = pl.ds(pl.multiple_of(t * tile, tile), tile)
        rkeys = lat[here, D_LAT : D_LAT + D_ROPE]
        rsum = jnp.zeros((tile, D_ROPE), F32)
        for h in range(heads):
            qn = q_ref[:, h * D_QK : h * D_QK + D_NOPE]
            qr = q_ref[:, h * D_QK + D_NOPE : (h + 1) * D_QK]
            prob = sc[h, here, :] * inv[h]
            ds = (prob * (dp[h, here, :] - delta[h]) * scale).astype(BF16)
            kv[here, h * D_NOPE : (h + 1) * D_NOPE] = nn(ds, qn).astype(BF16)
            at = heads * D_NOPE + h * D_V
            kv[here, at : at + D_V] = nn(prob.astype(BF16), do_ref[:, h * D_V : (h + 1) * D_V]).astype(BF16)
            rsum = rsum + nn(ds, qr)
            dqs[h, :, :D_NOPE] += tn(ds, kk[here, h * D_NOPE : (h + 1) * D_NOPE])
            dqs[h, :, D_NOPE:D_QK] += tn(ds, rkeys)
        rope[here, :] = rsum
        return carry

    lax.fori_loop(0, tiles, grads, 0)

    for c in range(D_LAT // LANE):
        up = tn(lat[:, c * LANE : (c + 1) * LANE], kv[...]).astype(BF16)
        gk[c * LANE : (c + 1) * LANE, :] = up[:, : heads * D_NOPE]
        gv[c * LANE : (c + 1) * LANE, :] = up[:, heads * D_NOPE :]

    share = D_LAT // nseq

    half_cols = heads * D_NOPE // 2

    def both(source, final, slots, order, c):
        cols = slice(c * half_cols, (c + 1) * half_cols)

        def rows_of(ref):
            return lambda part: ref.at[pl.ds(pl.multiple_of(part * share, share), share), cols]

        yield from reduce_steps(
            sems, seq, order, on_seq, rows_of(source), lambda k: slots.at[k, :, cols]
        )
        done = rows_of(final)(seq)
        done[...] = rows_of(source)(seq)[...]
        yield from gather_steps(sems, seq, order[::-1], on_seq, rows_of(final))

    def latent_grads():
        sub = rows // nhead

        def fold(part, carry):
            here = at_rows(part)
            total = nt(kv[here, : heads * D_NOPE], ku_ref[...])
            total = total + nt(kv[here, heads * D_NOPE :], vu_ref[...])
            for a in range(nhead):
                cut = slice(a * sub, (a + 1) * sub)
                lb[a, part, :, :D_LAT] = total[cut].astype(BF16)
                lb[a, part, :, D_LAT : D_LAT + D_ROPE] = rope[
                    pl.ds(pl.multiple_of(part * rows + a * sub, sub), sub), :
                ].astype(BF16)
            return carry

        lb[:, :, :, D_LAT:] = jnp.zeros(lb.shape[:3] + (lb.shape[3] - D_LAT,), BF16)
        lax.fori_loop(0, nseq, fold, 0)
        yield from reduce_steps(sems, head, head_bits, on_head, lambda a: lb.at[a], lambda k: rh.at[k])
        mine = lb.at[head]
        yield from reduce_steps(sems, seq, seq_bits, on_seq, lambda s: mine.at[s], lambda k: rl.at[k])
        fl[head] = lb[head, seq]
        yield from gather_steps(sems, head, head_bits[::-1], on_head, lambda a: fl.at[a])

    pipes = [
        both(gv, fv, rv, seq_bits[1:] + seq_bits[:1], 0),
        both(gk, fk, rk, seq_bits, 0),
        both(gv, fv, rv, seq_bits[1:] + seq_bits[:1], 1),
        both(gk, fk, rk, seq_bits, 1),
        latent_grads(),
    ]
    first = True
    while pipes:
        left = []
        for pipe in pipes:
            try:
                next(pipe)
                left.append(pipe)
            except StopIteration:
                pass
        pipes = left
        if first:
            first = False
            for h in range(heads):
                dq_ref[:, h * D_QK : (h + 1) * D_QK] = dqs[h, :, :D_QK].astype(BF16)
    dk_ref[...] = fk[...]
    dv_ref[...] = fv[...]
    sub = rows // nhead
    for a in range(nhead):
        dl_ref[a * sub : (a + 1) * sub, :] = fl[a, :, : D_LAT + D_ROPE]
    for copy in sems.sent:
        copy.wait_send()


def make_shards(nseq, nhead):
    def shards(queries, latents, key_up, value_up, out_grad, positions):
        rows, heads = latents.shape[0], key_up.shape[1] // D_NOPE
        qrows = queries.shape[0]
        count = rows * nseq
        width = -(-(D_LAT + D_ROPE + 2) // LANE) * LANE
        high, low = positions // LANE, positions % LANE
        coded = jnp.stack([high, low], axis=1).astype(BF16)
        packed = jnp.concatenate(
            [latents, coded, jnp.zeros((rows, width - D_LAT - D_ROPE - 2), BF16)], axis=1
        )
        qpos = positions.astype(F32)[None, :]
        up_cols = heads * D_NOPE
        share = D_LAT // nseq
        sub = rows // nhead
        copies = 4 * (nseq - 1) + 8 * (nseq - 1) + (nseq - 1) + 2 * (nhead - 1)
        vmem = pl.BlockSpec(memory_space=pltpu.VMEM)
        body = lambda *refs: kernel(nseq, nhead, *refs)
        dq, dl, dk, dv = pl.pallas_call(
            body,
            out_shape=(
                jax.ShapeDtypeStruct(queries.shape, BF16),
                jax.ShapeDtypeStruct(latents.shape, BF16),
                jax.ShapeDtypeStruct(key_up.shape, BF16),
                jax.ShapeDtypeStruct(value_up.shape, BF16),
            ),
            in_specs=[vmem] * 6,
            out_specs=(vmem,) * 4,
            scratch_shapes=[
                pltpu.VMEM((count, width), BF16),
                pltpu.VMEM((count, up_cols), BF16),
                pltpu.VMEM((count, up_cols), BF16),
                pltpu.VMEM((heads, count, qrows), F32),
                pltpu.VMEM((heads, count, qrows), F32),
                pltpu.VMEM((heads, qrows), F32),
                pltpu.VMEM((count, 2 * up_cols), BF16),
                pltpu.VMEM((count, D_ROPE), F32),
                pltpu.VMEM((D_LAT, up_cols), BF16),
                pltpu.VMEM((D_LAT, up_cols), BF16),
                pltpu.VMEM((D_LAT, up_cols), BF16),
                pltpu.VMEM((D_LAT, up_cols), BF16),
                pltpu.VMEM((nseq - 1, share, up_cols), BF16),
                pltpu.VMEM((nseq - 1, share, up_cols), BF16),
                pltpu.VMEM((nhead, nseq, sub, width), BF16),
                pltpu.VMEM((nhead - 1, nseq, sub, width), BF16),
                pltpu.VMEM((nseq - 1, sub, width), BF16),
                pltpu.VMEM((nhead, sub, width), BF16),
                pltpu.VMEM((heads, qrows, 2 * LANE), F32),
                pltpu.SemaphoreType.DMA((copies,)),
                pltpu.SemaphoreType.DMA((copies,)),
            ],
            compiler_params=pltpu.CompilerParams(
                collective_id=0, has_side_effects=True, vmem_limit_bytes=60 * 1024 * 1024
            ),
        )(queries, packed, key_up, value_up, out_grad, qpos)
        return dq, dl.astype(F32), dk.astype(F32), dv.astype(F32)

    return shards


def solution(mesh):
    in_specs = (
        P("seq", "head"),
        P("seq", None),
        P(None, "head"),
        P(None, "head"),
        P("seq", "head"),
        P("seq"),
    )
    out_specs = (P("seq", "head"), P("seq", None), P(None, "head"), P(None, "head"))
    shards = make_shards(mesh.shape["seq"], mesh.shape["head"])
    return jax.shard_map(shards, mesh=mesh, in_specs=in_specs, out_specs=out_specs, check_vma=False)
```

profile of v0, /device:TPU:0, one launch (start us, length us, event | category | flops | bytes accessed | tf_op | source)
XLA Modules:
  0.0 77.6 jit_solution(15204154763870282477)
XLA Ops:
  0.6 1.2 %convert_bitcast_fusion = (f32[1,128]{1,0:T(1,128)}, bf16[128,1]{0,1:T(2,128)(2,1)S(1)}, bf16[128,1]{0,1:T(2,128)(2,1)S(1)}) fusion(s32[128]{0:T(128)} %param.11), kind=kLoop, calls=%fused_computation.8 | loop fusion | flops 2816 | bytes 1536 | tf_op jit(solution)/shard_map/broadcast_in_dim | solution.py:345
  1.9 0.1 copy.11
  2.0 0.1 copy.12
  2.1 1.1 %copy.10 = bf16[128,576]{1,0:T(8,128)(2,1)S(1)} copy(bf16[128,576]{0,1:T(8,128)(2,1)} %param.7) | data formatting | bytes 294912 | tf_op args[1]
  3.2 0.1 pad.3.clone
  3.3 0.8 maximum_maximum_fusion.refs_1_
  4.1 68.6 %shard_map.93 = (bf16[128,768]{1,0:T(8,128)(2,1)}, bf16[128,576]{1,0:T(8,128)(2,1)}, bf16[512,512]{1,0:T(8,128)(2,1)}, bf16[512,512]{1,0:T(8,128)(2,1)}) custom-call(bf16[128,768]{1,0:T(8,128)(2,1)} %refs_0_.1, bf16[128,640]{1,0:T(8,128)(2,1)} %maximum_maximum_fusion.refs_1_, bf16[512,512]{1,0:T(8,128)(2,1)} %refs_2_.1, bf16[512,512]{1,0:T(8,128)(2,1)} %refs_3_.1, ...), custom_call_target="tpu_custom_call" | custom-call | tf_op jit(solution)/shard_map/pallas_call | solution.py:352
  72.7 0.0 copy-start
  72.7 2.2 %convert_element_type.15 = f32[512,512]{1,0:T(8,128)} convert(bf16[512,512]{1,0:T(8,128)(2,1)} %get-tuple-element.10) | non-fusion elementwise | flops 262144 | bytes 1572864 | tf_op jit(solution)/shard_map/convert_element_type | solution.py:389
  74.9 0.0 copy-done
  74.9 0.0 copy-start.2
  74.9 1.1 %convert_element_type.16 = f32[512,512]{1,0:T(8,128)} convert(bf16[512,512]{1,0:T(8,128)(2,1)S(1)} %copy-done) | non-fusion elementwise | flops 262144 | bytes 1572864 | tf_op jit(solution)/shard_map/convert_element_type | solution.py:389
  76.0 0.0 copy-done.2
  76.0 0.0 copy-start.1
  76.0 0.8 %copy.13 = f32[128,576]{0,1:T(8,128)} copy(bf16[128,576]{1,0:T(8,128)(2,1)S(1)} %copy-done.2) | data formatting | bytes 442368
  76.8 0.1 copy-done.1
  76.9 0.7 copy.15
  (1 shorter events, 0.0 us)
Async XLA Ops:
  72.7 2.2 %copy-start = (bf16[512,512]{1,0:T(8,128)(2,1)S(1)}, bf16[512,512]{1,0:T(8,128)(2,1)}, u32[]{:S(2)}) copy-start(bf16[512,512]{1,0:T(8,128)(2,1)} %get-tuple-element.11) | copy-start | bytes 1572868
  74.9 1.1 %copy-start.2 = (bf16[128,576]{1,0:T(8,128)(2,1)S(1)}, bf16[128,576]{1,0:T(8,128)(2,1)}, u32[]{:S(2)}) copy-start(bf16[128,576]{1,0:T(8,128)(2,1)} %get-tuple-element.9) | copy-start | bytes 442372
  76.0 0.9 %copy-start.1 = (bf16[128,768]{1,0:T(8,128)(2,1)S(1)}, bf16[128,768]{1,0:T(8,128)(2,1)}, u32[]{:S(2)}) copy-start(bf16[128,768]{1,0:T(8,128)(2,1)} %get-tuple-element.23) | copy-start | bytes 589828
where the time goes:
time: 77.9 us; the launch traced here: 77.6 us
  Pallas kernels  68.6 us (88%)
  other arithmetic  5.31 us (7%)
  local copies, waits for them, and re-layouts  3.02 us (4%)
    pallas_call x1, Pallas kernels, shards(): pl.pallas_call(body, out_shape=(jax.ShapeDtypeStruct(queries.shape, BF16)...  68.6 us
    convert_element_type x2, other arithmetic, shards(): return (dq, dl.astype(F32), dk.astype(F32), dv.astype(F32))  3.3 us
    unnamed x9, local copies, waits for them, and re-layouts  2.67 us

commit v1 on v0

v1 whole, which is shorter than its diff:
```python
import itertools
import math

import jax
import jax.numpy as jnp
from jax import lax
from jax.experimental import pallas as pl
from jax.experimental.pallas import tpu as pltpu
from jax.sharding import PartitionSpec as P

D_LAT = 512
D_ROPE = 64
D_NOPE = 128
D_V = 128
D_QK = D_NOPE + D_ROPE
D_ALL = D_LAT + D_ROPE
LANE = 128
STRIPE = 128
NEG = -1e30
LOG2E = 1.4426950408889634
MESH = pl.DeviceIdType.MESH
F32 = jnp.float32
BF16 = jnp.bfloat16


def bit(index, b):
    return (index // (1 << b)) % 2


def flip(index, b):
    return index + (1 << b) * (1 - 2 * bit(index, b))


def xor(index, mask):
    b = 0
    while mask >> b:
        if (mask >> b) & 1:
            index = flip(index, b)
        b += 1
    return index


def pick(index, bits):
    out = 0
    for k, b in enumerate(bits):
        out = out + (1 << k) * bit(index, b)
    return out


def put(index, bits, value):
    for k, b in enumerate(bits):
        index = index + (1 << b) * (((value >> k) & 1) - bit(index, b))
    return index


def nn(a, b):
    return lax.dot_general(a, b, (((1,), (0,)), ((), ())), preferred_element_type=F32)


def nt(a, b):
    return lax.dot_general(a, b, (((1,), (1,)), ((), ())), preferred_element_type=F32)


def loop(n, body, init):
    if n <= 8:
        for t in range(n):
            init = body(t, init)
        return init
    return lax.fori_loop(0, n, body, init)


class Sems:
    def __init__(self, send, recv):
        self.send, self.recv, self.used = send, recv, 0
        self.sent = []

    def copy(self, src, dst, device):
        k = self.used
        self.used += 1
        copy = pltpu.make_async_remote_copy(
            src_ref=src,
            dst_ref=dst,
            send_sem=self.send.at[k],
            recv_sem=self.recv.at[k],
            device_id=device,
            device_id_type=MESH,
        )
        copy.start()
        self.sent.append(copy)
        return copy


def kernel(
    nseq, nhead, subs,
    q_ref, lat_ref, ku_ref, vu_ref, do_ref, pos_ref,
    dq_ref, dl_ref, dk_ref, dv_ref,
    stage, qd, qall, dall, lat, pos, kt, vt, kuv, ut, sc, dp, mx, sinv, sdel,
    pr, ds, kvg, rp, up, ur, fin, lg, rc, ry, rx, ac, rz, fl, dqt, dqr,
    send, recv,
):
    seq, head = lax.axis_index("seq"), lax.axis_index("head")
    rows = lat_ref.shape[1]
    heads = ku_ref.shape[1] // D_NOPE
    nq, nk = heads * rows, nseq * rows
    nb = nseq.bit_length() - 1
    hb = heads.bit_length() - 1
    member_bits = [0] + list(range(nb - hb + 1, nb))
    group_bits = [b for b in range(nb) if b not in member_bits]
    groups = 1 << len(group_bits)
    nz = nseq // 2
    sub = D_ALL // nhead
    scale = 1.0 / math.sqrt(D_QK)
    sems = Sems(send, recv)
    u, w = pick(seq, member_bits), pick(seq, group_bits)
    x, z = bit(seq, 0), seq // 2
    core, y = bit(head, 0), bit(head, 1)

    def on_seq(s):
        return (s, head)

    def on_head(h):
        return (seq, h)

    other = on_head(flip(head, 0))
    across = on_head(flip(head, 1))

    barrier = pltpu.get_barrier_semaphore()
    for mask in range(1, nseq):
        pl.semaphore_signal(barrier, inc=1, device_id=on_seq(xor(seq, mask)), device_id_type=MESH)
    for device in (other, across):
        pl.semaphore_signal(barrier, inc=1, device_id=device, device_id_type=MESH)

    def at(start, size, step):
        return pl.ds(pl.multiple_of(start * step, step), size)

    for h in range(heads):
        stage[h, :D_QK, :] = q_ref[:, h * D_QK : (h + 1) * D_QK].T
        stage[h, D_QK:, :] = do_ref[:, h * D_V : (h + 1) * D_V].T
    lat[:, at(seq, rows, rows)] = lat_ref[...]
    pos[seq] = pos_ref[...]
    qd[:, at(u, rows, rows)] = stage[u]
    kuv[:, :D_NOPE] = ku_ref[:, at(u, D_NOPE, D_NOPE)]
    kuv[:, D_NOPE:] = vu_ref[:, at(u, D_V, D_V)]
    ut[...] = kuv[...].T
    mx[...] = jnp.full(mx.shape, NEG, F32)

    pl.semaphore_wait(barrier, nseq + 1)

    def gather(order, region, own, arrived):
        pending = {}

        def forward(mask):
            last = max([k for k, b in enumerate(order) if (mask >> b) & 1], default=-1)
            piece = region(xor(seq, mask))
            for b in order[last + 1 :]:
                pending[mask | (1 << b)] = sems.copy(
                    own if mask == 0 else piece, piece, on_seq(flip(seq, b))
                )

        forward(0)
        masks = [
            sum(1 << b for b in some)
            for size in range(1, len(order) + 1)
            for some in itertools.combinations(order, size)
        ]
        for mask in masks:
            yield
            pending[mask].wait_recv()
            forward(mask)
            arrived(mask)

    half = D_ALL // 2
    zbits = list(range(nb - 1, 0, -1))
    passes = {}

    def lat_region(s):
        return lat.at[at(core, half, half), at(s, rows, rows)]

    def pass_on(mask):
        piece = lat_region(xor(seq, mask))
        passes[mask] = sems.copy(piece, piece, other)

    lats = gather(zbits + [0], lat_region, lat_ref.at[at(core, half, half)], pass_on)
    next(lats)
    pos_in = [
        sems.copy(pos_ref, pos.at[seq], on_seq(xor(seq, mask))) for mask in range(1, nseq)
    ]
    q_in = []
    for v in range(1, heads):
        mask = sum(((v >> k) & 1) << b for k, b in enumerate(member_bits))
        there = xor(seq, mask)
        q_in.append(
            sems.copy(stage.at[pick(there, member_bits)], qd.at[:, at(u, rows, rows)], on_seq(there))
        )

    def keys_of(s):
        here = at(s, rows, rows)
        both = nn(ut[...], lat[:D_LAT, here]).astype(BF16)
        kt[:D_NOPE, here] = both[:D_NOPE]
        vt[:, here] = both[D_NOPE:]
        kt[D_NOPE:, here] = lat[D_LAT:, here]

    down = lax.broadcasted_iota(jnp.int32, (STRIPE, rows), 0)
    along = lax.broadcasted_iota(jnp.int32, (1, STRIPE), 1)
    per = rows // STRIPE

    def scores_of(s):
        here = at(s, rows, rows)
        keys, vals = kt[:, here], vt[:, here]
        rel = pos[s] - down
        for t in range(nq // STRIPE):
            part = slice(t * STRIPE, (t + 1) * STRIPE)
            cut = (t % per) * STRIPE
            first = pos[put(seq, member_bits, t // per)][:, cut : cut + STRIPE] - along
            first = jnp.concatenate([first] * per, axis=1)
            got = jnp.where(rel <= first, nn(qall[part, :], keys), NEG)
            sc[part, here] = got
            dp[part, here] = nn(dall[part, :], vals)
            top = mx[part, :]
            for c in range(rows // LANE):
                top = jnp.maximum(top, got[:, c * LANE : (c + 1) * LANE])
            mx[part, :] = top

    keys_of(seq)
    for copy in q_in:
        copy.wait_recv()
    qall[...] = qd[:D_QK, :].T
    dall[...] = qd[D_QK:, :].T
    for copy in pos_in:
        copy.wait_recv()
    scores_of(seq)
    order = zbits + [0]
    masks = [
        sum(1 << b for b in some)
        for size in range(1, len(order) + 1)
        for some in itertools.combinations(order, size)
    ]
    ready = []
    for mask in masks:
        next(lats, None)
        ready.append(mask)
        if len(ready) > 2:
            block = ready.pop(0)
            passes[block].wait_recv()
            keys_of(xor(seq, block))
            scores_of(xor(seq, block))
    for block in ready:
        passes[block].wait_recv()
        keys_of(xor(seq, block))
        scores_of(xor(seq, block))

    factor = scale * LOG2E
    for t in range(nq // STRIPE):
        part = slice(t * STRIPE, (t + 1) * STRIPE)
        top = jnp.max(mx[part, :], axis=1, keepdims=True) * factor

        def sums(k, carry):
            total, weighted = carry
            here = at(k, LANE, LANE)
            e = jnp.exp2(sc[part, here] * factor - top)
            sc[part, here] = e
            return total + e, weighted + e * dp[part, here]

        zero = jnp.zeros((STRIPE, LANE), F32)
        total, weighted = loop(nk // LANE, sums, (zero, zero))
        total = jnp.sum(total, axis=1, keepdims=True)
        weighted = jnp.sum(weighted, axis=1, keepdims=True)
        inv = 1.0 / total
        sinv[part, :] = jnp.broadcast_to(inv, (STRIPE, LANE))
        sdel[part, :] = jnp.broadcast_to(weighted * inv, (STRIPE, LANE))

        def norm(k, carry):
            here = at(k, LANE, LANE)
            prob = sc[part, here] * sinv[part, :]
            sc[part, here] = prob
            pr[part, here] = prob.astype(BF16)
            return carry

        loop(nk // LANE, norm, 0)

    tile = math.gcd(nk, 512)

    def values_grad(k, carry):
        here = at(k, tile, tile)
        kvg[D_NOPE:, here] = nn(qd[D_QK:, :], pr[:, here]).astype(BF16)
        return carry

    loop(nk // tile, values_grad, 0)
    up[0] = nt(lat[:D_LAT, :], kvg[D_NOPE:, :]).astype(BF16)

    share = D_LAT // groups
    piece = share // subs

    def up_pipe(a, i, order, out_ref):
        bits = group_bits[::-1]
        slot = 0
        source = lambda g: up.at[a, at(g * subs + i, piece, piece)]
        for k, b in enumerate(bits):
            rest = bits[k + 1 :]
            copies = []
            for values in itertools.product((0, 1), repeat=len(rest)):
                to, mine = flip(seq, b), seq
                for r, value in zip(rest, values):
                    to = to + (1 << r) * (value - bit(to, r))
                    mine = mine + (1 << r) * (value - bit(mine, r))
                copy = sems.copy(
                    source(pick(to, group_bits)), ur.at[a, i, slot], on_seq(flip(seq, b))
                )
                copies.append((copy, slot, pick(mine, group_bits)))
                slot += 1
            yield
            for copy, got, g in copies:
                copy.wait_recv()
                kept = source(g)
                kept[...] = (kept[...].astype(F32) + ur[a, i, got].astype(F32)).astype(BF16)

        def place(s):
            return (
                at(pick(s, group_bits) * subs + i, piece, piece),
                at(pick(s, member_bits), LANE, LANE),
            )

        def arrived(mask):
            r, c = place(xor(seq, mask))
            out_ref[r, c] = fin[a, r, c].astype(F32)

        r, c = place(seq)
        out_ref[r, c] = source(w)[...].astype(F32)

        def region(s):
            r, c = place(s)
            return fin.at[a, r, c]

        yield from gather(order, region, source(w), arrived)

    def start(pipes):
        return [p for p in pipes if next(p, "end") != "end"]

    ag = zbits + [0]
    live = start([up_pipe(0, i, ag, dv_ref) for i in range(subs)])

    for t in range(nq // STRIPE):
        part = slice(t * STRIPE, (t + 1) * STRIPE)

        def scored(k, carry):
            here = at(k, LANE, LANE)
            ds[part, here] = (
                sc[part, here] * (dp[part, here] - sdel[part, :]) * scale
            ).astype(BF16)
            return carry

        loop(nk // LANE, scored, 0)

    def keys_grad(k, carry):
        here = at(k, tile, tile)
        got = nn(qd[:D_QK, :], ds[:, here]).astype(BF16)
        kvg[:D_NOPE, here] = got[:D_NOPE]
        rp[:, here] = got[D_NOPE:]
        return carry

    loop(nk // tile, keys_grad, 0)
    up[1] = nt(lat[:D_LAT, :], kvg[:D_NOPE, :]).astype(BF16)
    live += start([up_pipe(1, i, ag, dk_ref) for i in range(subs)])

    zmasks = list(range(1, nz))[::-1] + [0]
    to_core, to_y, to_x, to_z = {}, {}, {}, {}
    mine, others = y * 2 + core, (1 - y) * 2 + core

    def fold(k):
        here = at(xor(z, k), 2 * rows, 2 * rows)
        got = nn(kuv[...], kvg[:, here]).astype(BF16)
        got = jnp.concatenate([got, rp[:, here]], axis=0)
        for h in range(nhead):
            lg[h, k] = got[h * sub : (h + 1) * sub]
        to_core[k] = [
            sems.copy(lg.at[t * 2 + 1 - core, k], rc.at[j, k], other)
            for j, t in ((0, 1 - y), (1, y))
        ]

    def add_core(k):
        to_core[k][0].wait_recv()
        lg[others, k] = (lg[others, k].astype(F32) + rc[0, k].astype(F32)).astype(BF16)
        to_y[k] = sems.copy(lg.at[others, k], ry.at[k], across)
        to_core[k][1].wait_recv()
        lg[mine, k] = (lg[mine, k].astype(F32) + rc[1, k].astype(F32)).astype(BF16)

    def add_y(k):
        to_y[k].wait_recv()
        lg[mine, k] = (lg[mine, k].astype(F32) + ry[k].astype(F32)).astype(BF16)
        to_x[k] = sems.copy(
            lg.at[mine, k, :, at(1 - x, rows, rows)], rx.at[k], on_seq(flip(seq, 0))
        )

    def add_x(k):
        to_x[k].wait_recv()
        kept = lg[mine, k, :, at(x, rows, rows)].astype(F32) + rx[k].astype(F32)
        ac[k] = kept.astype(BF16)
        if k:
            to_z[k] = sems.copy(ac.at[k], rz.at[k], on_seq(xor(seq, 2 * k)))

    def lat_pipe():
        for stage_of in (add_core, add_y, add_x):
            for k in zmasks:
                stage_of(k)
                yield
        total = ac[0].astype(F32)
        for k in zmasks[:-1]:
            to_z[k].wait_recv()
            total = total + rz[k].astype(F32)
        fl[head] = total.astype(BF16)
        first = sems.copy(fl.at[head], fl.at[head], across)
        second = sems.copy(fl.at[head], fl.at[head], other)
        yield
        first.wait_recv()
        third = sems.copy(fl.at[others], fl.at[others], other)
        second.wait_recv()
        yield
        third.wait_recv()
        for h in range(nhead):
            dl_ref[h * sub : (h + 1) * sub, :] = fl[h].astype(F32)

    for k in zmasks:
        fold(k)
    live = start(live)
    dqt[...] = nt(kt[...], ds[...]).astype(BF16)
    dq_in = []
    for v in range(1, heads):
        mask = sum(((v >> k) & 1) << b for k, b in enumerate(member_bits))
        there = xor(seq, mask)
        dq_in.append(
            sems.copy(
                dqt.at[:, at(pick(there, member_bits), rows, rows)], dqr.at[u], on_seq(there)
            )
        )
    dqr[u] = dqt[:, at(u, rows, rows)]
    live = start(live + [lat_pipe()])

    def dq_pipe():
        for _ in range(6):
            yield
        for copy in dq_in:
            copy.wait_recv()
        for h in range(heads):
            dq_ref[:, h * D_QK : (h + 1) * D_QK] = dqr[h].T

    live += start([dq_pipe()])
    while live:
        live = start(live)
    for copy in sems.sent:
        copy.wait_send()


def make_shards(nseq, nhead):
    def shards(queries, latents, key_up, value_up, out_grad, positions):
        rows, heads = latents.shape[0], key_up.shape[1] // D_NOPE
        nq, nk = heads * rows, nseq * rows
        nz, groups = nseq // 2, nseq // heads
        subs = 2
        share = D_LAT // groups
        sub = D_ALL // nhead
        cols = key_up.shape[1]
        copies = (nseq - 1) * 3 + 2 * (heads - 1)
        copies += 2 * subs * (groups - 1 + nseq - 1) + 5 * nz + 3
        vmem = pl.BlockSpec(memory_space=pltpu.VMEM)
        body = lambda *refs: kernel(nseq, nhead, subs, *refs)
        scratch = [
            ((heads, D_QK + D_V, rows), BF16),
            ((D_QK + D_V, nq), BF16),
            ((nq, D_QK), BF16),
            ((nq, D_V), BF16),
            ((D_ALL, nk), BF16),
            ((nseq, 1, rows), jnp.int32),
            ((D_QK, nk), BF16),
            ((D_V, nk), BF16),
            ((D_LAT, D_NOPE + D_V), BF16),
            ((D_NOPE + D_V, D_LAT), BF16),
            ((nq, nk), F32),
            ((nq, nk), F32),
            ((nq, LANE), F32),
            ((nq, LANE), F32),
            ((nq, LANE), F32),
            ((nq, nk), BF16),
            ((nq, nk), BF16),
            ((D_NOPE + D_V, nk), BF16),
            ((D_ROPE, nk), BF16),
            ((2, D_LAT, LANE), BF16),
            ((2, subs, max(groups - 1, 1), share // subs, LANE), BF16),
            ((2, D_LAT, cols), BF16),
            ((nhead, nz, sub, 2 * rows), BF16),
            ((nhead // 2, nz, sub, 2 * rows), BF16),
            ((nz, sub, 2 * rows), BF16),
            ((nz, sub, rows), BF16),
            ((nz, sub, rows), BF16),
            ((nz, sub, rows), BF16),
            ((nhead, sub, rows), BF16),
            ((D_QK, nq), BF16),
            ((heads, D_QK, rows), BF16),
        ]
        limit = 8 * 1024 * 1024
        for shape, dtype in scratch:
            padded = (-(-shape[-1] // LANE) * LANE) * (-(-shape[-2] // 16) * 16)
            limit += math.prod(shape[:-2]) * padded * jnp.dtype(dtype).itemsize
        dq, dl, dk, dv = pl.pallas_call(
            body,
            out_shape=(
                jax.ShapeDtypeStruct(queries.shape, BF16),
                jax.ShapeDtypeStruct((D_ALL, rows), F32),
                jax.ShapeDtypeStruct(key_up.shape, F32),
                jax.ShapeDtypeStruct(value_up.shape, F32),
            ),
            in_specs=[vmem] * 6,
            out_specs=(vmem,) * 4,
            scratch_shapes=[pltpu.VMEM(shape, dtype) for shape, dtype in scratch]
            + [pltpu.SemaphoreType.DMA((copies,)), pltpu.SemaphoreType.DMA((copies,))],
            compiler_params=pltpu.CompilerParams(
                collective_id=0, has_side_effects=True, vmem_limit_bytes=min(limit, 60 * 1024 * 1024)
            ),
        )(queries, latents.T, key_up, value_up, out_grad, positions[None, :])
        return dq, dl.T, dk, dv

    return shards


def solution(mesh):
    in_specs = (
        P("seq", "head"),
        P("seq", None),
        P(None, "head"),
        P(None, "head"),
        P("seq", "head"),
        P("seq"),
    )
    out_specs = (P("seq", "head"), P("seq", None), P(None, "head"), P(None, "head"))
    shards = make_shards(mesh.shape["seq"], mesh.shape["head"])
    return jax.shard_map(shards, mesh=mesh, in_specs=in_specs, out_specs=out_specs, check_vma=False)
```

time: 77.9 us -> 69.8 us (0.90)
  Pallas kernels: 68.6 us -> 60.1 us
  local copies, waits for them, and re-layouts: 3.02 us -> 8.8 us
  other arithmetic: 5.31 us -> 0 us
    pallas_call x1, Pallas kernels: 68.6 us -> 60.1 us  [shards(): pl.pallas_call(body, out_shape=(jax.ShapeDtypeStruct(queries.shape, BF16)...]
    unnamed x9 -> x16, local copies, waits for them, and re-layouts: 2.67 us -> 8.8 us
    convert_element_type x2 -> x0, other arithmetic: 3.3 us -> none  [shards(): return (dq, dl.astype(F32), dk.astype(F32), dv.astype(F32))]
    broadcast_in_dim x1 -> x0, other arithmetic: 1.24 us -> none  [shards(): qpos = positions.astype(F32)[None, :]]
where the time goes in v1:
time: 69.8 us; the launch traced here: 69.5 us
  Pallas kernels  60.1 us (86%)
  local copies, waits for them, and re-layouts  8.8 us (13%)
    pallas_call x1, Pallas kernels, shards(): pl.pallas_call(body, out_shape=(jax.ShapeDtypeStruct(queries.shape, BF16)...  60.1 us
    unnamed x16, local copies, waits for them, and re-layouts  8.8 us

profile of v1, /device:TPU:0, one launch (start us, length us, event | category | flops | bytes accessed | tf_op | source)
XLA Modules:
  0.0 69.5 jit_solution(8662747861353819014)
XLA Ops:
  0.6 0.0 copy-start.5
  0.6 0.6 copy-done.5
  1.3 0.0 copy-start
  1.3 1.0 %copy-done = bf16[512,512]{1,0:T(8,128)(2,1)S(1)} copy-done((bf16[512,512]{1,0:T(8,128)(2,1)S(1)}, bf16[512,512]{1,0:T(8,128)(2,1)}, u32[]{:S(2)}) %copy-start) | copy-done | bytes 524312
  2.3 0.0 copy-start.1
  2.3 1.0 %copy-done.1 = bf16[512,512]{1,0:T(8,128)(2,1)S(1)} copy-done((bf16[512,512]{1,0:T(8,128)(2,1)S(1)}, bf16[512,512]{1,0:T(8,128)(2,1)}, u32[]{:S(2)}) %copy-start.1) | copy-done | bytes 524312
  3.4 0.0 copy-start.2
  3.4 0.9 %copy-done.2 = bf16[128,768]{1,0:T(8,128)(2,1)S(1)} copy-done((bf16[128,768]{1,0:T(8,128)(2,1)S(1)}, bf16[128,768]{1,0:T(8,128)(2,1)}, u32[]{:S(2)}) %copy-start.2) | copy-done | bytes 196632
  4.3 0.0 copy-start.3
  4.3 0.9 %copy-done.3 = bf16[128,576]{0,1:T(8,128)(2,1)S(1)} copy-done((bf16[128,576]{0,1:T(8,128)(2,1)S(1)}, bf16[128,576]{0,1:T(8,128)(2,1)}, u32[]{:S(2)}) %copy-start.3) | copy-done | bytes 147480
  5.2 0.0 copy-start.4
  5.2 0.9 %copy-done.4 = bf16[128,512]{1,0:T(8,128)(2,1)S(1)} copy-done((bf16[128,512]{1,0:T(8,128)(2,1)S(1)}, bf16[128,512]{1,0:T(8,128)(2,1)}, u32[]{:S(2)}) %copy-start.4) | copy-done | bytes 131096
  6.1 60.1 %shard_map.93 = (bf16[128,768]{1,0:T(8,128)(2,1)S(1)}, f32[576,128]{1,0:T(8,128)S(1)}, f32[512,512]{1,0:T(8,128)S(1)}, f32[512,512]{1,0:T(8,128)S(1)}) custom-call(bf16[128,768]{1,0:T(8,128)(2,1)S(1)} %copy-done.2, bf16[576,128]{1,0:T(8,128)(2,1)S(1)} %bitcast.4, bf16[512,512]{1,0:T(8,128)(2,1)S(1)} %copy-done, bf16[512,512]{1,0:T(8,128)(2,1)S(1)} %copy-done.1, ...), custom_call_target="tpu_custom_call" | custom-call | tf_op jit(solution)/shard_map/pallas_call | solution.py:503
  66.2 0.7 copy.14
  66.9 0.7 %copy.15 = f32[128,576]{0,1:T(8,128)} copy(f32[128,576]{0,1:T(8,128)S(1)} %bitcast.3) | data formatting | bytes 589824
  67.6 1.0 %copy.16 = f32[512,512]{1,0:T(8,128)} copy(f32[512,512]{1,0:T(8,128)S(1)} %get-tuple-element.18) | data formatting | bytes 2097152
  68.6 1.0 %copy.17 = f32[512,512]{1,0:T(8,128)} copy(f32[512,512]{1,0:T(8,128)S(1)} %get-tuple-element.19) | data formatting | bytes 2097152
Async XLA Ops:
  0.6 0.7 copy-start.5
  1.3 1.0 %copy-start = (bf16[512,512]{1,0:T(8,128)(2,1)S(1)}, bf16[512,512]{1,0:T(8,128)(2,1)}, u32[]{:S(2)}) copy-start(bf16[512,512]{1,0:T(8,128)(2,1)} %refs_2_.1) | copy-start | bytes 1572868
  2.3 1.0 %copy-start.1 = (bf16[512,512]{1,0:T(8,128)(2,1)S(1)}, bf16[512,512]{1,0:T(8,128)(2,1)}, u32[]{:S(2)}) copy-start(bf16[512,512]{1,0:T(8,128)(2,1)} %refs_3_.1) | copy-start | bytes 1572868
  3.4 0.9 %copy-start.2 = (bf16[128,768]{1,0:T(8,128)(2,1)S(1)}, bf16[128,768]{1,0:T(8,128)(2,1)}, u32[]{:S(2)}) copy-start(bf16[128,768]{1,0:T(8,128)(2,1)} %refs_0_.1) | copy-start | bytes 589828
  4.3 0.9 %copy-start.3 = (bf16[128,576]{0,1:T(8,128)(2,1)S(1)}, bf16[128,576]{0,1:T(8,128)(2,1)}, u32[]{:S(2)}) copy-start(bf16[128,576]{0,1:T(8,128)(2,1)} %param.7) | copy-start | bytes 442372
  5.2 0.9 %copy-start.4 = (bf16[128,512]{1,0:T(8,128)(2,1)S(1)}, bf16[128,512]{1,0:T(8,128)(2,1)}, u32[]{:S(2)}) copy-start(bf16[128,512]{1,0:T(8,128)(2,1)} %refs_4_.1) | copy-start | bytes 393220

commit v2 on v1

--- a/solution.py
+++ b/solution.py
@@ -92,15 +92,16 @@
 
 def kernel(
     nseq, nhead, subs,
-    q_ref, lat_ref, ku_ref, vu_ref, do_ref, pos_ref,
+    q_in, lat_in, ku_in, vu_in, do_in, pos_in,
     dq_ref, dl_ref, dk_ref, dv_ref,
+    q_ref, lat_ref, do_ref, pos_ref, load,
     stage, qd, qall, dall, lat, pos, kt, vt, kuv, ut, sc, dp, mx, sinv, sdel,
     pr, ds, kvg, rp, up, ur, fin, lg, rc, ry, rx, ac, rz, fl, dqt, dqr,
     send, recv,
 ):
     seq, head = lax.axis_index("seq"), lax.axis_index("head")
-    rows = lat_ref.shape[1]
-    heads = ku_ref.shape[1] // D_NOPE
+    rows = lat_in.shape[1]
+    heads = ku_in.shape[1] // D_NOPE
     nq, nk = heads * rows, nseq * rows
     nb = nseq.bit_length() - 1
     hb = heads.bit_length() - 1
@@ -133,16 +134,30 @@
     def at(start, size, step):
         return pl.ds(pl.multiple_of(start * step, step), size)
 
+    mine_k, mine_v = at(u, D_NOPE, D_NOPE), at(u, D_V, D_V)
+    loads = [
+        pltpu.make_async_copy(src, dst, load.at[k])
+        for k, (src, dst) in enumerate((
+            (lat_in, lat_ref),
+            (q_in, q_ref),
+            (do_in, do_ref),
+            (pos_in, pos_ref),
+            (ku_in.at[:, mine_k], kuv.at[:, :D_NOPE]),
+            (vu_in.at[:, mine_v], kuv.at[:, D_NOPE:]),
+        ))
+    ]
+    for copy in loads:
+        copy.start()
+    mx[...] = jnp.full(mx.shape, NEG, F32)
+    for copy in loads:
+        copy.wait()
     for h in range(heads):
         stage[h, :D_QK, :] = q_ref[:, h * D_QK : (h + 1) * D_QK].T
         stage[h, D_QK:, :] = do_ref[:, h * D_V : (h + 1) * D_V].T
     lat[:, at(seq, rows, rows)] = lat_ref[...]
     pos[seq] = pos_ref[...]
     qd[:, at(u, rows, rows)] = stage[u]
-    kuv[:, :D_NOPE] = ku_ref[:, at(u, D_NOPE, D_NOPE)]
-    kuv[:, D_NOPE:] = vu_ref[:, at(u, D_V, D_V)]
     ut[...] = kuv[...].T
-    mx[...] = jnp.full(mx.shape, NEG, F32)
 
     pl.semaphore_wait(barrier, nseq + 1)
 
@@ -182,14 +197,14 @@
 
     lats = gather(zbits + [0], lat_region, lat_ref.at[at(core, half, half)], pass_on)
     next(lats)
-    pos_in = [
+    pos_got = [
         sems.copy(pos_ref, pos.at[seq], on_seq(xor(seq, mask))) for mask in range(1, nseq)
     ]
-    q_in = []
+    q_got = []
     for v in range(1, heads):
         mask = sum(((v >> k) & 1) << b for k, b in enumerate(member_bits))
         there = xor(seq, mask)
-        q_in.append(
+        q_got.append(
             sems.copy(stage.at[pick(there, member_bits)], qd.at[:, at(u, rows, rows)], on_seq(there))
         )
 
@@ -222,11 +237,11 @@
             mx[part, :] = top
 
     keys_of(seq)
-    for copy in q_in:
+    for copy in q_got:
         copy.wait_recv()
     qall[...] = qd[:D_QK, :].T
     dall[...] = qd[D_QK:, :].T
-    for copy in pos_in:
+    for copy in pos_got:
         copy.wait_recv()
     scores_of(seq)
     order = zbits + [0]
@@ -450,6 +465,15 @@
         copy.wait_send()
 
 
+def store(*refs):
+    sems = refs[8]
+    copies = [pltpu.make_async_copy(refs[k], refs[4 + k], sems.at[k]) for k in range(4)]
+    for copy in copies:
+        copy.start()
+    for copy in copies:
+        copy.wait()
+
+
 def make_shards(nseq, nhead):
     def shards(queries, latents, key_up, value_up, out_grad, positions):
         rows, heads = latents.shape[0], key_up.shape[1] // D_NOPE
@@ -463,6 +487,12 @@
         copies += 2 * subs * (groups - 1 + nseq - 1) + 5 * nz + 3
         vmem = pl.BlockSpec(memory_space=pltpu.VMEM)
         body = lambda *refs: kernel(nseq, nhead, subs, *refs)
+        moved = [
+            (queries.shape, BF16),
+            ((D_ALL, rows), BF16),
+            (out_grad.shape, BF16),
+            ((1, rows), jnp.int32),
+        ]
         scratch = [
             ((heads, D_QK + D_V, rows), BF16),
             ((D_QK + D_V, nq), BF16),
@@ -497,7 +527,7 @@
             ((heads, D_QK, rows), BF16),
         ]
         limit = 8 * 1024 * 1024
-        for shape, dtype in scratch:
+        for shape, dtype in moved + scratch:
             padded = (-(-shape[-1] // LANE) * LANE) * (-(-shape[-2] // 16) * 16)
             limit += math.prod(shape[:-2]) * padded * jnp.dtype(dtype).itemsize
         dq, dl, dk, dv = pl.pallas_call(
@@ -508,14 +538,28 @@
                 jax.ShapeDtypeStruct(key_up.shape, F32),
                 jax.ShapeDtypeStruct(value_up.shape, F32),
             ),
-            in_specs=[vmem] * 6,
+            in_specs=[pl.BlockSpec(memory_space=pltpu.HBM)] * 6,
             out_specs=(vmem,) * 4,
-            scratch_shapes=[pltpu.VMEM(shape, dtype) for shape, dtype in scratch]
+            scratch_shapes=[pltpu.VMEM(shape, dtype) for shape, dtype in moved]
+            + [pltpu.SemaphoreType.DMA((6,))]
+            + [pltpu.VMEM(shape, dtype) for shape, dtype in scratch]
             + [pltpu.SemaphoreType.DMA((copies,)), pltpu.SemaphoreType.DMA((copies,))],
             compiler_params=pltpu.CompilerParams(
                 collective_id=0, has_side_effects=True, vmem_limit_bytes=min(limit, 60 * 1024 * 1024)
             ),
-        )(queries, latents.T, key_up, value_up, out_grad, positions[None, :])
+        )(*[
+            pltpu.with_memory_space_constraint(a, pltpu.HBM)
+            for a in (queries, latents.T, key_up, value_up, out_grad, positions[None, :])
+        ])
+        done = (dq, dl, dk, dv)
+        dq, dl, dk, dv = pl.pallas_call(
+            store,
+            out_shape=[jax.ShapeDtypeStruct(a.shape, a.dtype) for a in done],
+            in_specs=[vmem] * 4,
+            out_specs=[pl.BlockSpec(memory_space=pltpu.HBM)] * 4,
+            scratch_shapes=[pltpu.SemaphoreType.DMA((4,))],
+            compiler_params=pltpu.CompilerParams(vmem_limit_bytes=1024 * 1024),
+        )(*done)
         return dq, dl.T, dk, dv
 
     return shards

time: 69.8 us -> 62.6 us (0.90)
  local copies, waits for them, and re-layouts: 8.8 us -> 0 us
  Pallas kernels: 60.1 us -> 61.7 us
    unnamed x16 -> x0, local copies, waits for them, and re-layouts: 8.8 us -> none
    pallas_call x0 -> x1, Pallas kernels: none -> 1.51 us  [shards(): pl.pallas_call(store, out_shape=[jax.ShapeDtypeStruct(a.shape, a.dtype) f...]
where the time goes in v2:
time: 62.6 us; the launch traced here: 62.4 us
  Pallas kernels  61.7 us (99%)
  between operations  0.64 us (1%)
    pallas_call x1, Pallas kernels, shards(): pl.pallas_call(body, out_shape=(jax.ShapeDtypeStruct(queries.shape, BF16)...  60.2 us
    pallas_call x1, Pallas kernels, shards(): pl.pallas_call(store, out_shape=[jax.ShapeDtypeStruct(a.shape, a.dtype) f...  1.51 us

profile of v2, /device:TPU:0, one launch (start us, length us, event | category | flops | bytes accessed | tf_op | source)
XLA Modules:
  0.0 62.4 jit_solution(10825338785610657162)
XLA Ops:
  0.6 60.2 %shard_map.93 = (bf16[128,768]{1,0:T(8,128)(2,1)S(1)}, f32[576,128]{1,0:T(8,128)S(1)}, f32[512,512]{1,0:T(8,128)S(1)}, f32[512,512]{1,0:T(8,128)S(1)}) custom-call(bf16[128,768]{1,0:T(8,128)(2,1)} %refs_0_.1, bf16[576,128]{1,0:T(8,128)(2,1)} %bitcast.3, bf16[512,512]{1,0:T(8,128)(2,1)} %refs_2_.1, bf16[512,512]{1,0:T(8,128)(2,1)} %refs_3_.1, ...), custom_call_target="tpu_custom_call" | custom-call | tf_op jit(solution)/shard_map/pallas_call | solution.py:533
  60.9 1.5 %shard_map.94 = (bf16[128,768]{1,0:T(8,128)(2,1)}, f32[576,128]{1,0:T(8,128)}, f32[512,512]{1,0:T(8,128)}, f32[512,512]{1,0:T(8,128)}) custom-call(bf16[128,768]{1,0:T(8,128)(2,1)S(1)} %get-tuple-element.12.refs_0_, f32[576,128]{1,0:T(8,128)S(1)} %get-tuple-element.13.refs_1_, f32[512,512]{1,0:T(8,128)S(1)} %get-tuple-element.14.refs_2_, ...), custom_call_target="tpu_custom_call" | custom-call | tf_op jit(solution)/shard_map/pallas_call | solution.py:555

commit v3 on v2

--- a/solution.py
+++ b/solution.py
@@ -109,7 +109,6 @@
     group_bits = [b for b in range(nb) if b not in member_bits]
     groups = 1 << len(group_bits)
     nz = nseq // 2
-    sub = D_ALL // nhead
     scale = 1.0 / math.sqrt(D_QK)
     sems = Sems(send, recv)
     u, w = pick(seq, member_bits), pick(seq, group_bits)
@@ -149,57 +148,48 @@
     for copy in loads:
         copy.start()
     mx[...] = jnp.full(mx.shape, NEG, F32)
-    for copy in loads:
+
+    zbits = list(range(nb - 1, 0, -1))
+    order = zbits + [0]
+    masks = [
+        sum(1 << b for b in some)
+        for size in range(1, nb + 1)
+        for some in itertools.combinations(order, size)
+    ]
+    levels = [[m for m in masks if m.bit_count() == size] for size in range(1, nb + 1)]
+    by_seq, by_core, by_y, by_both = {}, {}, {}, {}
+    sub = D_ALL // nhead
+
+    def quarter(h, s):
+        return lat.at[at(h, sub, sub), at(s, rows, rows)]
+
+    def forward(mask):
+        last = max([k for k, b in enumerate(order) if (mask >> b) & 1], default=-1)
+        piece = quarter(head, xor(seq, mask))
+        for b in order[last + 1 :]:
+            source = piece if mask else lat_ref.at[at(head, sub, sub)]
+            by_seq[mask | (1 << b)] = sems.copy(source, piece, on_seq(flip(seq, b)))
+
+    def relay(mask):
+        by_seq[mask].wait_recv()
+        forward(mask)
+        piece = quarter(head, xor(seq, mask))
+        by_y[mask] = sems.copy(piece, piece, across)
+        by_core[mask] = sems.copy(piece, piece, other)
+
+    def relay_y(mask):
+        by_y[mask].wait_recv()
+        piece = quarter(flip(head, 1), xor(seq, mask))
+        by_both[mask] = sems.copy(piece, piece, other)
+
+    loads[0].wait()
+    pl.semaphore_wait(barrier, nseq + 1)
+    forward(0)
+    for copy in loads[1:4]:
         copy.wait()
     for h in range(heads):
         stage[h, :D_QK, :] = q_ref[:, h * D_QK : (h + 1) * D_QK].T
         stage[h, D_QK:, :] = do_ref[:, h * D_V : (h + 1) * D_V].T
-    lat[:, at(seq, rows, rows)] = lat_ref[...]
-    pos[seq] = pos_ref[...]
-    qd[:, at(u, rows, rows)] = stage[u]
-    ut[...] = kuv[...].T
-
-    pl.semaphore_wait(barrier, nseq + 1)
-
-    def gather(order, region, own, arrived):
-        pending = {}
-
-        def forward(mask):
-            last = max([k for k, b in enumerate(order) if (mask >> b) & 1], default=-1)
-            piece = region(xor(seq, mask))
-            for b in order[last + 1 :]:
-                pending[mask | (1 << b)] = sems.copy(
-                    own if mask == 0 else piece, piece, on_seq(flip(seq, b))
-                )
-
-        forward(0)
-        masks = [
-            sum(1 << b for b in some)
-            for size in range(1, len(order) + 1)
-            for some in itertools.combinations(order, size)
-        ]
-        for mask in masks:
-            yield
-            pending[mask].wait_recv()
-            forward(mask)
-            arrived(mask)
-
-    half = D_ALL // 2
-    zbits = list(range(nb - 1, 0, -1))
-    passes = {}
-
-    def lat_region(s):
-        return lat.at[at(core, half, half), at(s, rows, rows)]
-
-    def pass_on(mask):
-        piece = lat_region(xor(seq, mask))
-        passes[mask] = sems.copy(piece, piece, other)
-
-    lats = gather(zbits + [0], lat_region, lat_ref.at[at(core, half, half)], pass_on)
-    next(lats)
-    pos_got = [
-        sems.copy(pos_ref, pos.at[seq], on_seq(xor(seq, mask))) for mask in range(1, nseq)
-    ]
     q_got = []
     for v in range(1, heads):
         mask = sum(((v >> k) & 1) << b for k, b in enumerate(member_bits))
@@ -207,6 +197,15 @@
         q_got.append(
             sems.copy(stage.at[pick(there, member_bits)], qd.at[:, at(u, rows, rows)], on_seq(there))
         )
+    pos_got = [
+        sems.copy(pos_ref, pos.at[seq], on_seq(xor(seq, mask))) for mask in range(1, nseq)
+    ]
+    for copy in loads[4:]:
+        copy.wait()
+    lat[:, at(seq, rows, rows)] = lat_ref[...]
+    pos[seq] = pos_ref[...]
+    qd[:, at(u, rows, rows)] = stage[u]
+    ut[...] = kuv[...].T
 
     def keys_of(s):
         here = at(s, rows, rows)
@@ -236,33 +235,36 @@
                 top = jnp.maximum(top, got[:, c * LANE : (c + 1) * LANE])
             mx[part, :] = top
 
+    def block_of(mask):
+        by_core[mask].wait_recv()
+        by_both[mask].wait_recv()
+        keys_of(xor(seq, mask))
+        scores_of(xor(seq, mask))
+
     keys_of(seq)
+    for mask in levels[0]:
+        relay(mask)
     for copy in q_got:
         copy.wait_recv()
     qall[...] = qd[:D_QK, :].T
     dall[...] = qd[D_QK:, :].T
+    for mask in levels[0]:
+        relay_y(mask)
     for copy in pos_got:
         copy.wait_recv()
     scores_of(seq)
-    order = zbits + [0]
-    masks = [
-        sum(1 << b for b in some)
-        for size in range(1, len(order) + 1)
-        for some in itertools.combinations(order, size)
-    ]
-    ready = []
-    for mask in masks:
-        next(lats, None)
-        ready.append(mask)
-        if len(ready) > 2:
-            block = ready.pop(0)
-            passes[block].wait_recv()
-            keys_of(xor(seq, block))
-            scores_of(xor(seq, block))
-    for block in ready:
-        passes[block].wait_recv()
-        keys_of(xor(seq, block))
-        scores_of(xor(seq, block))
+    for mask in levels[1]:
+        relay(mask)
+    for mask in levels[0]:
+        block_of(mask)
+    for k in range(1, nb):
+        if k + 1 < nb:
+            for mask in levels[k + 1]:
+                relay(mask)
+        for mask in levels[k]:
+            relay_y(mask)
+        for mask in levels[k]:
+            block_of(mask)
 
     factor = scale * LOG2E
     for t in range(nq // STRIPE):
@@ -306,53 +308,68 @@
     share = D_LAT // groups
     piece = share // subs
 
-    def up_pipe(a, i, order, out_ref):
+    summed, moved = {}, {}
+
+    def source(a, i, g):
+        return up.at[a, at(g * subs + i, piece, piece)]
+
+    def place(i, s):
+        return (
+            at(pick(s, group_bits) * subs + i, piece, piece),
+            at(pick(s, member_bits), LANE, LANE),
+        )
+
+    def sum_start(a, i, k=0, slot=0):
         bits = group_bits[::-1]
+        if k == len(bits):
+            return
+        b, rest = bits[k], bits[k + 1 :]
+        summed[a, i] = []
+        for values in itertools.product((0, 1), repeat=len(rest)):
+            to, own = flip(seq, b), seq
+            for r, value in zip(rest, values):
+                to = to + (1 << r) * (value - bit(to, r))
+                own = own + (1 << r) * (value - bit(own, r))
+            copy = sems.copy(
+                source(a, i, pick(to, group_bits)), ur.at[a, i, slot], on_seq(flip(seq, b))
+            )
+            summed[a, i].append((copy, slot, pick(own, group_bits)))
+            slot += 1
+
+    def sum_end(a, i):
         slot = 0
-        source = lambda g: up.at[a, at(g * subs + i, piece, piece)]
-        for k, b in enumerate(bits):
-            rest = bits[k + 1 :]
-            copies = []
-            for values in itertools.product((0, 1), repeat=len(rest)):
-                to, mine = flip(seq, b), seq
-                for r, value in zip(rest, values):
-                    to = to + (1 << r) * (value - bit(to, r))
-                    mine = mine + (1 << r) * (value - bit(mine, r))
-                copy = sems.copy(
-                    source(pick(to, group_bits)), ur.at[a, i, slot], on_seq(flip(seq, b))
-                )
-                copies.append((copy, slot, pick(mine, group_bits)))
-                slot += 1
-            yield
-            for copy, got, g in copies:
+        for k in range(len(group_bits)):
+            for copy, slot, g in summed[a, i]:
                 copy.wait_recv()
-                kept = source(g)
-                kept[...] = (kept[...].astype(F32) + ur[a, i, got].astype(F32)).astype(BF16)
-
-        def place(s):
-            return (
-                at(pick(s, group_bits) * subs + i, piece, piece),
-                at(pick(s, member_bits), LANE, LANE),
+                kept = source(a, i, g)
+                kept[...] = (kept[...].astype(F32) + ur[a, i, slot].astype(F32)).astype(BF16)
+            sum_start(a, i, k + 1, slot + 1)
+
+    def spread(a, i, mask, bits):
+        r, c = place(i, xor(seq, mask))
+        piece_at = fin.at[a, r, c]
+        for b in bits:
+            moved[a, i, mask | (1 << b)] = sems.copy(
+                piece_at if mask else source(a, i, w), piece_at, on_seq(flip(seq, b))
             )
 
-        def arrived(mask):
-            r, c = place(xor(seq, mask))
-            out_ref[r, c] = fin[a, r, c].astype(F32)
-
-        r, c = place(seq)
-        out_ref[r, c] = source(w)[...].astype(F32)
-
-        def region(s):
-            r, c = place(s)
-            return fin.at[a, r, c]
-
-        yield from gather(order, region, source(w), arrived)
-
-    def start(pipes):
-        return [p for p in pipes if next(p, "end") != "end"]
-
-    ag = zbits + [0]
-    live = start([up_pipe(0, i, ag, dv_ref) for i in range(subs)])
+    def spread_z(a, i, mask):
+        last = max([k for k, b in enumerate(zbits) if (mask >> b) & 1], default=-1)
+        spread(a, i, mask, zbits[last + 1 :])
+
+    def spread_x(a, i, mask):
+        spread(a, i, mask, [0])
+
+    def arrive(a, i, mask):
+        moved[a, i, mask].wait_recv()
+
+    def finish(a, i, mask):
+        r, c = place(i, xor(seq, mask))
+        got = fin[a, r, c] if mask else source(a, i, w)[...]
+        (dk_ref if a else dv_ref)[r, c] = got.astype(F32)
+
+    for i in range(subs):
+        sum_start(0, i)
 
     for t in range(nq // STRIPE):
         part = slice(t * STRIPE, (t + 1) * STRIPE)
@@ -375,7 +392,8 @@
 
     loop(nk // tile, keys_grad, 0)
     up[1] = nt(lat[:D_LAT, :], kvg[:D_NOPE, :]).astype(BF16)
-    live += start([up_pipe(1, i, ag, dk_ref) for i in range(subs)])
+    for i in range(subs):
+        sum_start(1, i)
 
     zmasks = list(range(1, nz))[::-1] + [0]
     to_core, to_y, to_x, to_z = {}, {}, {}, {}
@@ -413,31 +431,25 @@
         if k:
             to_z[k] = sems.copy(ac.at[k], rz.at[k], on_seq(xor(seq, 2 * k)))
 
-    def lat_pipe():
-        for stage_of in (add_core, add_y, add_x):
-            for k in zmasks:
-                stage_of(k)
-                yield
-        total = ac[0].astype(F32)
-        for k in zmasks[:-1]:
-            to_z[k].wait_recv()
-            total = total + rz[k].astype(F32)
-        fl[head] = total.astype(BF16)
-        first = sems.copy(fl.at[head], fl.at[head], across)
-        second = sems.copy(fl.at[head], fl.at[head], other)
-        yield
-        first.wait_recv()
-        third = sems.copy(fl.at[others], fl.at[others], other)
-        second.wait_recv()
-        yield
-        third.wait_recv()
-        for h in range(nhead):
-            dl_ref[h * sub : (h + 1) * sub, :] = fl[h].astype(F32)
+    chunks = [(a, i) for a in range(2) for i in range(subs)]
+    values, keys = chunks[:subs], chunks[subs:]
+    zmoves = [m for m in masks if not m & 1]
+    near_z = [m for m in zmoves if m.bit_count() == 1]
+    far_z = [m for m in zmoves if m.bit_count() > 1]
 
     for k in zmasks:
         fold(k)
-    live = start(live)
+    for a, i in values:
+        sum_end(a, i)
+        spread_z(a, i, 0)
+        spread_x(a, i, 0)
     dqt[...] = nt(kt[...], ds[...]).astype(BF16)
+    for a, i in keys:
+        sum_end(a, i)
+        spread_z(a, i, 0)
+        spread_x(a, i, 0)
+    for k in zmasks:
+        add_core(k)
     dq_in = []
     for v in range(1, heads):
         mask = sum(((v >> k) & 1) << b for k, b in enumerate(member_bits))
@@ -448,19 +460,60 @@
             )
         )
     dqr[u] = dqt[:, at(u, rows, rows)]
-    live = start(live + [lat_pipe()])
-
-    def dq_pipe():
-        for _ in range(6):
-            yield
-        for copy in dq_in:
-            copy.wait_recv()
-        for h in range(heads):
-            dq_ref[:, h * D_QK : (h + 1) * D_QK] = dqr[h].T
-
-    live += start([dq_pipe()])
-    while live:
-        live = start(live)
+    for chunk in chunks:
+        finish(*chunk, 0)
+    late = []
+    for k, mask in enumerate(near_z):
+        for chunk in chunks:
+            arrive(*chunk, mask)
+            spread_z(*chunk, mask)
+            if k == 0:
+                spread_x(*chunk, mask)
+            else:
+                late.append((*chunk, mask))
+            finish(*chunk, mask)
+    for k in zmasks[:-1]:
+        add_y(k)
+    for k in zmasks[:1]:
+        add_x(k)
+    for move in late[: len(late) // 2]:
+        spread_x(*move)
+    late = late[len(late) // 2 :]
+    for k in zmasks[-1:]:
+        add_y(k)
+    for k in zmasks[1:-1]:
+        add_x(k)
+    for mask in far_z:
+        for chunk in chunks:
+            arrive(*chunk, mask)
+            spread_z(*chunk, mask)
+            late.append((*chunk, mask))
+    for move in late:
+        spread_x(*move)
+        if move[2] in far_z:
+            finish(*move)
+    add_x(0)
+    total = ac[0].astype(F32)
+    for k in zmasks[:-1]:
+        to_z[k].wait_recv()
+        total = total + rz[k].astype(F32)
+    fl[head] = total.astype(BF16)
+    first = sems.copy(fl.at[head], fl.at[head], across)
+    second = sems.copy(fl.at[head], fl.at[head], other)
+    for copy in dq_in:
+        copy.wait_recv()
+    for h in range(heads):
+        dq_ref[:, h * D_QK : (h + 1) * D_QK] = dqr[h].T
+    first.wait_recv()
+    third = sems.copy(fl.at[others], fl.at[others], other)
+    for mask in [0] + zmoves:
+        for chunk in chunks:
+            arrive(*chunk, mask | 1)
+            finish(*chunk, mask | 1)
+    second.wait_recv()
+    third.wait_recv()
+    for h in range(nhead):
+        dl_ref[h * sub : (h + 1) * sub, :] = fl[h].astype(F32)
     for copy in sems.sent:
         copy.wait_send()
 
@@ -483,7 +536,7 @@
         share = D_LAT // groups
         sub = D_ALL // nhead
         cols = key_up.shape[1]
-        copies = (nseq - 1) * 3 + 2 * (heads - 1)
+        copies = (nseq - 1) * 5 + 2 * (heads - 1)
         copies += 2 * subs * (groups - 1 + nseq - 1) + 5 * nz + 3
         vmem = pl.BlockSpec(memory_space=pltpu.VMEM)
         body = lambda *refs: kernel(nseq, nhead, subs, *refs)

time: 62.6 us -> 54.9 us (0.88)
  Pallas kernels: 61.7 us -> 54.1 us
    pallas_call x1, Pallas kernels: 60.2 us -> 52.6 us  [shards(): pl.pallas_call(body, out_shape=(jax.ShapeDtypeStruct(queries.shape, BF16)...]
where the time goes in v3:
time: 54.9 us; the launch traced here: 54.8 us
  Pallas kernels  54.1 us (99%)
  between operations  0.64 us (1%)
    pallas_call x1, Pallas kernels, shards(): pl.pallas_call(body, out_shape=(jax.ShapeDtypeStruct(queries.shape, BF16)...  52.6 us
    pallas_call x1, Pallas kernels, shards(): pl.pallas_call(store, out_shape=[jax.ShapeDtypeStruct(a.shape, a.dtype) f...  1.51 us

profile of v3, /device:TPU:0, one launch (start us, length us, event | category | flops | bytes accessed | tf_op | source)
XLA Modules:
  0.0 54.8 jit_solution(8847542938232172515)
XLA Ops:
  0.6 52.6 %shard_map.93 = (bf16[128,768]{1,0:T(8,128)(2,1)S(1)}, f32[576,128]{1,0:T(8,128)S(1)}, f32[512,512]{1,0:T(8,128)S(1)}, f32[512,512]{1,0:T(8,128)S(1)}) custom-call(bf16[128,768]{1,0:T(8,128)(2,1)} %refs_0_.1, bf16[576,128]{1,0:T(8,128)(2,1)} %bitcast.3, bf16[512,512]{1,0:T(8,128)(2,1)} %refs_2_.1, bf16[512,512]{1,0:T(8,128)(2,1)} %refs_3_.1, ...), custom_call_target="tpu_custom_call" | custom-call | tf_op jit(solution)/shard_map/pallas_call | solution.py:586
  53.2 1.5 %shard_map.94 = (bf16[128,768]{1,0:T(8,128)(2,1)}, f32[576,128]{1,0:T(8,128)}, f32[512,512]{1,0:T(8,128)}, f32[512,512]{1,0:T(8,128)}) custom-call(bf16[128,768]{1,0:T(8,128)(2,1)S(1)} %get-tuple-element.12.refs_0_, f32[576,128]{1,0:T(8,128)S(1)} %get-tuple-element.13.refs_1_, f32[512,512]{1,0:T(8,128)S(1)} %get-tuple-element.14.refs_2_, ...), custom_call_target="tpu_custom_call" | custom-call | tf_op jit(solution)/shard_map/pallas_call | solution.py:608

commit v4 on v3

--- a/solution.py
+++ b/solution.py
@@ -69,12 +69,19 @@
     return lax.fori_loop(0, n, body, init)
 
 
+def when(only, act):
+    if only is None:
+        act()
+    else:
+        pl.when(only)(act)
+
+
 class Sems:
     def __init__(self, send, recv):
         self.send, self.recv, self.used = send, recv, 0
         self.sent = []
 
-    def copy(self, src, dst, device):
+    def copy(self, src, dst, device, only=None):
         k = self.used
         self.used += 1
         copy = pltpu.make_async_remote_copy(
@@ -85,8 +92,8 @@
             device_id=device,
             device_id_type=MESH,
         )
-        copy.start()
-        self.sent.append(copy)
+        when(only, copy.start)
+        self.sent.append((only, copy))
         return copy
 
 
@@ -96,7 +103,7 @@
     dq_ref, dl_ref, dk_ref, dv_ref,
     q_ref, lat_ref, do_ref, pos_ref, load,
     stage, qd, qall, dall, lat, pos, kt, vt, kuv, ut, sc, dp, mx, sinv, sdel,
-    pr, ds, kvg, rp, up, ur, fin, lg, rc, ry, rx, ac, rz, fl, dqt, dqr,
+    pr, ds, kvg, rp, up, ur, ug, fin, lg, rc, ry, rx, ac, rz, fl, dqt, dqr,
     send, recv,
 ):
     seq, head = lax.axis_index("seq"), lax.axis_index("head")
@@ -105,15 +112,16 @@
     nq, nk = heads * rows, nseq * rows
     nb = nseq.bit_length() - 1
     hb = heads.bit_length() - 1
-    member_bits = [0] + list(range(nb - hb + 1, nb))
-    group_bits = [b for b in range(nb) if b not in member_bits]
+    slot_bits = list(range(1, 1 + hb))
+    group_bits = list(range(1 + hb, nb))
     groups = 1 << len(group_bits)
     nz = nseq // 2
     scale = 1.0 / math.sqrt(D_QK)
     sems = Sems(send, recv)
-    u, w = pick(seq, member_bits), pick(seq, group_bits)
+    u, w = pick(seq, slot_bits), pick(seq, group_bits)
     x, z = bit(seq, 0), seq // 2
     core, y = bit(head, 0), bit(head, 1)
+    active, passive = core == x, core != x
 
     def on_seq(s):
         return (s, head)
@@ -129,6 +137,16 @@
         pl.semaphore_signal(barrier, inc=1, device_id=on_seq(xor(seq, mask)), device_id_type=MESH)
     for device in (other, across):
         pl.semaphore_signal(barrier, inc=1, device_id=device, device_id_type=MESH)
+
+    def swap(k):
+        return (xor(seq, 2 * k) + core - x, head + x - core)
+
+    def greet(k):
+        pl.semaphore_signal(barrier, inc=1, device_id=swap(k), device_id_type=MESH)
+
+    for k in range(1, heads):
+        greet(k)
+    when(passive, lambda: greet(0))
 
     def at(start, size, step):
         return pl.ds(pl.multiple_of(start * step, step), size)
@@ -145,8 +163,10 @@
             (vu_in.at[:, mine_v], kuv.at[:, D_NOPE:]),
         ))
     ]
-    for copy in loads:
+    for copy in loads[:4]:
         copy.start()
+    for copy in loads[4:]:
+        when(active, copy.start)
     mx[...] = jnp.full(mx.shape, NEG, F32)
 
     zbits = list(range(nb - 1, 0, -1))
@@ -156,7 +176,7 @@
         for size in range(1, nb + 1)
         for some in itertools.combinations(order, size)
     ]
-    levels = [[m for m in masks if m.bit_count() == size] for size in range(1, nb + 1)]
+    zmoves = [m for m in masks if not m & 1]
     by_seq, by_core, by_y, by_both = {}, {}, {}, {}
     sub = D_ALL // nhead
 
@@ -164,15 +184,15 @@
         return lat.at[at(h, sub, sub), at(s, rows, rows)]
 
     def forward(mask):
-        last = max([k for k, b in enumerate(order) if (mask >> b) & 1], default=-1)
         piece = quarter(head, xor(seq, mask))
-        for b in order[last + 1 :]:
-            source = piece if mask else lat_ref.at[at(head, sub, sub)]
-            by_seq[mask | (1 << b)] = sems.copy(source, piece, on_seq(flip(seq, b)))
+        source = piece if mask else lat_ref.at[at(head, sub, sub)]
+        for to in [1] if mask else zmoves + [1]:
+            by_seq[mask | to] = sems.copy(source, piece, on_seq(xor(seq, to)))
 
     def relay(mask):
         by_seq[mask].wait_recv()
-        forward(mask)
+        if not mask & 1:
+            forward(mask)
         piece = quarter(head, xor(seq, mask))
         by_y[mask] = sems.copy(piece, piece, across)
         by_core[mask] = sems.copy(piece, piece, other)
@@ -183,29 +203,34 @@
         by_both[mask] = sems.copy(piece, piece, other)
 
     loads[0].wait()
-    pl.semaphore_wait(barrier, nseq + 1)
+    pl.semaphore_wait(barrier, nseq + heads + (core - x) * (core - x))
     forward(0)
-    for copy in loads[1:4]:
+    loads[3].wait()
+    pos_got = [
+        sems.copy(pos_ref, pos.at[seq], on_seq(xor(seq, mask))) for mask in range(1, nseq)
+    ]
+    for copy in loads[1:3]:
         copy.wait()
     for h in range(heads):
         stage[h, :D_QK, :] = q_ref[:, h * D_QK : (h + 1) * D_QK].T
         stage[h, D_QK:, :] = do_ref[:, h * D_V : (h + 1) * D_V].T
-    q_got = []
-    for v in range(1, heads):
-        mask = sum(((v >> k) & 1) << b for k, b in enumerate(member_bits))
-        there = xor(seq, mask)
-        q_got.append(
-            sems.copy(stage.at[pick(there, member_bits)], qd.at[:, at(u, rows, rows)], on_seq(there))
+    q_got = {}
+    for k in range(heads):
+        q_got[k] = sems.copy(
+            stage.at[pick(xor(seq, 2 * k), slot_bits)],
+            qd.at[:, at(u, rows, rows)],
+            swap(k),
+            None if k else passive,
         )
-    pos_got = [
-        sems.copy(pos_ref, pos.at[seq], on_seq(xor(seq, mask))) for mask in range(1, nseq)
-    ]
     for copy in loads[4:]:
-        copy.wait()
+        when(active, copy.wait)
+    kuv_got = sems.copy(kuv, kuv, other, active)
     lat[:, at(seq, rows, rows)] = lat_ref[...]
     pos[seq] = pos_ref[...]
-    qd[:, at(u, rows, rows)] = stage[u]
-    ut[...] = kuv[...].T
+
+    @pl.when(active)
+    def _():
+        qd[:, at(u, rows, rows)] = stage[u]
 
     def keys_of(s):
         here = at(s, rows, rows)
@@ -215,19 +240,20 @@
         kt[D_NOPE:, here] = lat[D_LAT:, here]
 
     down = lax.broadcasted_iota(jnp.int32, (STRIPE, rows), 0)
-    along = lax.broadcasted_iota(jnp.int32, (1, STRIPE), 1)
     per = rows // STRIPE
-
-    def scores_of(s):
+    lane = jnp.concatenate([lax.broadcasted_iota(jnp.int32, (1, STRIPE), 1)] * per, axis=1)
+
+    def scores_of(s, k):
         here = at(s, rows, rows)
         keys, vals = kt[:, here], vt[:, here]
         rel = pos[s] - down
-        for t in range(nq // STRIPE):
-            part = slice(t * STRIPE, (t + 1) * STRIPE)
-            cut = (t % per) * STRIPE
-            first = pos[put(seq, member_bits, t // per)][:, cut : cut + STRIPE] - along
-            first = jnp.concatenate([first] * per, axis=1)
-            got = jnp.where(rel <= first, nn(qall[part, :], keys), NEG)
+        first = pos[xor(seq, 2 * k) + core - x] - lane
+        slot = pick(xor(seq, 2 * k), slot_bits)
+        for t in range(per):
+            part = at(slot * per + t, STRIPE, STRIPE)
+            base = first[:, t * STRIPE : (t + 1) * STRIPE]
+            base = jnp.concatenate([base] * per, axis=1)
+            got = jnp.where(rel <= base, nn(qall[part, :], keys), NEG)
             sc[part, here] = got
             dp[part, here] = nn(dall[part, :], vals)
             top = mx[part, :]
@@ -235,36 +261,63 @@
                 top = jnp.maximum(top, got[:, c * LANE : (c + 1) * LANE])
             mx[part, :] = top
 
+    def turn(k):
+        if k:
+            q_got[k].wait_recv()
+        else:
+            when(passive, q_got[0].wait_recv)
+        here = at(pick(xor(seq, 2 * k), slot_bits), rows, rows)
+        qall[here, :] = qd[:D_QK, here].T
+        dall[here, :] = qd[D_QK:, here].T
+
     def block_of(mask):
         by_core[mask].wait_recv()
         by_both[mask].wait_recv()
         keys_of(xor(seq, mask))
-        scores_of(xor(seq, mask))
-
+
+    for mask in zmoves + [1]:
+        relay(mask)
+    when(passive, kuv_got.wait_recv)
+    ut[...] = kuv[...].T
     keys_of(seq)
-    for mask in levels[0]:
-        relay(mask)
-    for copy in q_got:
-        copy.wait_recv()
-    qall[...] = qd[:D_QK, :].T
-    dall[...] = qd[D_QK:, :].T
-    for mask in levels[0]:
+    for mask in zmoves:
+        relay(mask | 1)
+    for mask in zmoves + [1]:
         relay_y(mask)
     for copy in pos_got:
         copy.wait_recv()
-    scores_of(seq)
-    for mask in levels[1]:
-        relay(mask)
-    for mask in levels[0]:
+    for k in range(heads // 2):
+        turn(k)
+    for mask in zmoves + [1]:
         block_of(mask)
-    for k in range(1, nb):
-        if k + 1 < nb:
-            for mask in levels[k + 1]:
-                relay(mask)
-        for mask in levels[k]:
-            relay_y(mask)
-        for mask in levels[k]:
-            block_of(mask)
+    for mask in zmoves:
+        relay_y(mask | 1)
+    early = [0] + zmoves + [1]
+    for mask in early:
+        for k in range(heads // 2):
+            scores_of(xor(seq, mask), k)
+    for mask in zmoves:
+        block_of(mask | 1)
+    for mask in zmoves:
+        for k in range(heads // 2):
+            scores_of(xor(seq, mask | 1), k)
+    for k in range(heads // 2, heads):
+        turn(k)
+        for mask in [0] + masks:
+            scores_of(xor(seq, mask), k)
+
+    first_sent, sems.sent = sems.sent, []
+
+    def drain(sent):
+        for only in (None, active, passive):
+            some = [copy for kind, copy in sent if kind is only]
+
+            def act():
+                for copy in some:
+                    copy.wait_send()
+
+            if some:
+                when(only, act)
 
     factor = scale * LOG2E
     for t in range(nq // STRIPE):
@@ -316,41 +369,51 @@
     def place(i, s):
         return (
             at(pick(s, group_bits) * subs + i, piece, piece),
-            at(pick(s, member_bits), LANE, LANE),
+            at(pick(s, slot_bits), LANE, LANE),
         )
 
-    def sum_start(a, i, k=0, slot=0):
-        bits = group_bits[::-1]
-        if k == len(bits):
-            return
-        b, rest = bits[k], bits[k + 1 :]
-        summed[a, i] = []
-        for values in itertools.product((0, 1), repeat=len(rest)):
-            to, own = flip(seq, b), seq
-            for r, value in zip(rest, values):
-                to = to + (1 << r) * (value - bit(to, r))
-                own = own + (1 << r) * (value - bit(own, r))
-            copy = sems.copy(
-                source(a, i, pick(to, group_bits)), ur.at[a, i, slot], on_seq(flip(seq, b))
-            )
-            summed[a, i].append((copy, slot, pick(own, group_bits)))
-            slot += 1
+    def sum_start(a, i):
+        for g in range(groups):
+            part = at(g * subs + i, piece, piece)
+            summed[a, i, g] = sems.copy(up.at[a, part], ur.at[a, part], other, passive)
+
+    def add_up(a, i, g, ref):
+        def act():
+            kept = source(a, i, g)
+            kept[...] = (kept[...].astype(F32) + ref[...].astype(F32)).astype(BF16)
+
+        when(active, act)
 
     def sum_end(a, i):
-        slot = 0
-        for k in range(len(group_bits)):
-            for copy, slot, g in summed[a, i]:
-                copy.wait_recv()
-                kept = source(a, i, g)
-                kept[...] = (kept[...].astype(F32) + ur[a, i, slot].astype(F32)).astype(BF16)
-            sum_start(a, i, k + 1, slot + 1)
+        for g in range(groups):
+            when(active, summed[a, i, g].wait_recv)
+            add_up(a, i, g, ur.at[a, at(g * subs + i, piece, piece)])
+        bits, slot = group_bits[::-1], 0
+        for k, b in enumerate(bits):
+            rest, copies = bits[k + 1 :], []
+            for values in itertools.product((0, 1), repeat=len(rest)):
+                to, own = flip(seq, b), seq
+                for r, value in zip(rest, values):
+                    to = to + (1 << r) * (value - bit(to, r))
+                    own = own + (1 << r) * (value - bit(own, r))
+                copy = sems.copy(
+                    source(a, i, pick(to, group_bits)),
+                    ug.at[a, i, slot],
+                    on_seq(flip(seq, b)),
+                    active,
+                )
+                copies.append((copy, slot, pick(own, group_bits)))
+                slot += 1
+            for copy, at_slot, g in copies:
+                when(active, copy.wait_recv)
+                add_up(a, i, g, ug.at[a, i, at_slot])
 
     def spread(a, i, mask, bits):
         r, c = place(i, xor(seq, mask))
         piece_at = fin.at[a, r, c]
         for b in bits:
             moved[a, i, mask | (1 << b)] = sems.copy(
-                piece_at if mask else source(a, i, w), piece_at, on_seq(flip(seq, b))
+                piece_at if mask else source(a, i, w), piece_at, on_seq(flip(seq, b)), active
             )
 
     def spread_z(a, i, mask):
@@ -361,12 +424,16 @@
         spread(a, i, mask, [0])
 
     def arrive(a, i, mask):
-        moved[a, i, mask].wait_recv()
+        when(passive if mask & 1 else active, moved[a, i, mask].wait_recv)
 
     def finish(a, i, mask):
         r, c = place(i, xor(seq, mask))
-        got = fin[a, r, c] if mask else source(a, i, w)[...]
-        (dk_ref if a else dv_ref)[r, c] = got.astype(F32)
+
+        def act():
+            got = fin[a, r, c] if mask else source(a, i, w)[...]
+            (dk_ref if a else dv_ref)[r, c] = got.astype(F32)
+
+        when(passive if mask & 1 else active, act)
 
     for i in range(subs):
         sum_start(0, i)
@@ -383,6 +450,10 @@
 
         loop(nk // LANE, scored, 0)
 
+    for i in range(subs):
+        sum_end(0, i)
+        spread_z(0, i, 0)
+        spread_x(0, i, 0)
     def keys_grad(k, carry):
         here = at(k, tile, tile)
         got = nn(qd[:D_QK, :], ds[:, here]).astype(BF16)
@@ -391,9 +462,6 @@
         return carry
 
     loop(nk // tile, keys_grad, 0)
-    up[1] = nt(lat[:D_LAT, :], kvg[:D_NOPE, :]).astype(BF16)
-    for i in range(subs):
-        sum_start(1, i)
 
     zmasks = list(range(1, nz))[::-1] + [0]
     to_core, to_y, to_x, to_z = {}, {}, {}, {}
@@ -433,65 +501,74 @@
 
     chunks = [(a, i) for a in range(2) for i in range(subs)]
     values, keys = chunks[:subs], chunks[subs:]
-    zmoves = [m for m in masks if not m & 1]
     near_z = [m for m in zmoves if m.bit_count() == 1]
     far_z = [m for m in zmoves if m.bit_count() > 1]
 
     for k in zmasks:
         fold(k)
-    for a, i in values:
-        sum_end(a, i)
-        spread_z(a, i, 0)
-        spread_x(a, i, 0)
-    dqt[...] = nt(kt[...], ds[...]).astype(BF16)
+    up[1] = nt(lat[:D_LAT, :], kvg[:D_NOPE, :]).astype(BF16)
+    for i in range(subs):
+        sum_start(1, i)
+    for k in zmasks:
+        add_core(k)
     for a, i in keys:
         sum_end(a, i)
         spread_z(a, i, 0)
         spread_x(a, i, 0)
-    for k in zmasks:
-        add_core(k)
-    dq_in = []
-    for v in range(1, heads):
-        mask = sum(((v >> k) & 1) << b for k, b in enumerate(member_bits))
-        there = xor(seq, mask)
-        dq_in.append(
-            sems.copy(
-                dqt.at[:, at(pick(there, member_bits), rows, rows)], dqr.at[u], on_seq(there)
-            )
-        )
-    dqr[u] = dqt[:, at(u, rows, rows)]
     for chunk in chunks:
         finish(*chunk, 0)
-    late = []
-    for k, mask in enumerate(near_z):
-        for chunk in chunks:
+
+    held = []
+
+    def along_z(some, mask, hold=False):
+        for chunk in some:
             arrive(*chunk, mask)
             spread_z(*chunk, mask)
-            if k == 0:
+            if hold:
+                held.append((*chunk, mask))
+            else:
                 spread_x(*chunk, mask)
-            else:
-                late.append((*chunk, mask))
             finish(*chunk, mask)
-    for k in zmasks[:-1]:
+
+    dqt[...] = nt(kt[...], ds[...]).astype(BF16)
+    for mask in near_z[1:][::-1]:
+        along_z(values, mask)
+    drain(first_sent)
+    for k in zmasks[:-3]:
         add_y(k)
+    for mask in near_z[1:][::-1]:
+        along_z(keys, mask)
+    for k in zmasks[-3:-2]:
+        add_y(k)
+    along_z(values, near_z[0])
+    for k in zmasks[-2:-1]:
+        add_y(k)
+    along_z(keys, near_z[0], True)
     for k in zmasks[:1]:
         add_x(k)
-    for move in late[: len(late) // 2]:
-        spread_x(*move)
-    late = late[len(late) // 2 :]
     for k in zmasks[-1:]:
         add_y(k)
+    for move in held:
+        spread_x(*move)
+    dq_in = [
+        sems.copy(
+            dqt.at[:, at(pick(xor(seq, 2 * k), slot_bits), rows, rows)],
+            dqr.at[u],
+            swap(k),
+            None if k else passive,
+        )
+        for k in range(heads)
+    ]
+
+    @pl.when(active)
+    def _():
+        dqr[u] = dqt[:, at(u, rows, rows)]
+
     for k in zmasks[1:-1]:
         add_x(k)
+    last_sent, sems.sent = sems.sent, []
     for mask in far_z:
-        for chunk in chunks:
-            arrive(*chunk, mask)
-            spread_z(*chunk, mask)
-            late.append((*chunk, mask))
-    for move in late:
-        spread_x(*move)
-        if move[2] in far_z:
-            finish(*move)
+        along_z(chunks, mask)
     add_x(0)
     total = ac[0].astype(F32)
     for k in zmasks[:-1]:
@@ -500,8 +577,10 @@
     fl[head] = total.astype(BF16)
     first = sems.copy(fl.at[head], fl.at[head], across)
     second = sems.copy(fl.at[head], fl.at[head], other)
-    for copy in dq_in:
+    drain(last_sent)
+    for copy in dq_in[1:]:
         copy.wait_recv()
+    when(passive, dq_in[0].wait_recv)
     for h in range(heads):
         dq_ref[:, h * D_QK : (h + 1) * D_QK] = dqr[h].T
     first.wait_recv()
@@ -514,8 +593,7 @@
     third.wait_recv()
     for h in range(nhead):
         dl_ref[h * sub : (h + 1) * sub, :] = fl[h].astype(F32)
-    for copy in sems.sent:
-        copy.wait_send()
+    drain(sems.sent)
 
 
 def store(*refs):
@@ -531,13 +609,13 @@
     def shards(queries, latents, key_up, value_up, out_grad, positions):
         rows, heads = latents.shape[0], key_up.shape[1] // D_NOPE
         nq, nk = heads * rows, nseq * rows
-        nz, groups = nseq // 2, nseq // heads
+        nz, groups = nseq // 2, nseq // (2 * heads)
         subs = 2
         share = D_LAT // groups
         sub = D_ALL // nhead
         cols = key_up.shape[1]
-        copies = (nseq - 1) * 5 + 2 * (heads - 1)
-        copies += 2 * subs * (groups - 1 + nseq - 1) + 5 * nz + 3
+        copies = (nseq - 1) * 5 + 2 * heads + 1
+        copies += 2 * subs * (2 * groups - 1 + nseq - 1) + 5 * nz + 3
         vmem = pl.BlockSpec(memory_space=pltpu.VMEM)
         body = lambda *refs: kernel(nseq, nhead, subs, *refs)
         moved = [
@@ -566,6 +644,7 @@
             ((nq, nk), BF16),
             ((D_NOPE + D_V, nk), BF16),
             ((D_ROPE, nk), BF16),
+            ((2, D_LAT, LANE), BF16),
             ((2, D_LAT, LANE), BF16),
             ((2, subs, max(groups - 1, 1), share // subs, LANE), BF16),
             ((2, D_LAT, cols), BF16),

time: 54.9 us -> 49.9 us (0.909)
  Pallas kernels: 54.1 us -> 48.7 us
    pallas_call x1, Pallas kernels: 52.6 us -> 47.2 us  [shards(): pl.pallas_call(body, out_shape=(jax.ShapeDtypeStruct(queries.shape, BF16)...]
where the time goes in v4:
time: 49.9 us; the launch traced here: 49.3 us
  Pallas kernels  48.7 us (98%)
  between operations  0.64 us (1%)
    pallas_call x1, Pallas kernels, shards(): pl.pallas_call(body, out_shape=(jax.ShapeDtypeStruct(queries.shape, BF16)...  47.2 us
    pallas_call x1, Pallas kernels, shards(): pl.pallas_call(store, out_shape=[jax.ShapeDtypeStruct(a.shape, a.dtype) f...  1.51 us

profile of v4, /device:TPU:0, one launch (start us, length us, event | category | flops | bytes accessed | tf_op | source)
XLA Modules:
  0.0 49.3 jit_solution(11511860021072954054)
XLA Ops:
  0.6 47.2 %shard_map.93 = (bf16[128,768]{1,0:T(8,128)(2,1)S(1)}, f32[576,128]{1,0:T(8,128)S(1)}, f32[512,512]{1,0:T(8,128)S(1)}, f32[512,512]{1,0:T(8,128)S(1)}) custom-call(bf16[128,768]{1,0:T(8,128)(2,1)} %refs_0_.1, bf16[576,128]{1,0:T(8,128)(2,1)} %bitcast.3, bf16[512,512]{1,0:T(8,128)(2,1)} %refs_2_.1, bf16[512,512]{1,0:T(8,128)(2,1)} %refs_3_.1, ...), custom_call_target="tpu_custom_call" | custom-call | tf_op jit(solution)/shard_map/pallas_call | solution.py:665
  47.8 1.5 %shard_map.94 = (bf16[128,768]{1,0:T(8,128)(2,1)}, f32[576,128]{1,0:T(8,128)}, f32[512,512]{1,0:T(8,128)}, f32[512,512]{1,0:T(8,128)}) custom-call(bf16[128,768]{1,0:T(8,128)(2,1)S(1)} %get-tuple-element.12.refs_0_, f32[576,128]{1,0:T(8,128)S(1)} %get-tuple-element.13.refs_1_, f32[512,512]{1,0:T(8,128)S(1)} %get-tuple-element.14.refs_2_, ...), custom_call_target="tpu_custom_call" | custom-call | tf_op jit(solution)/shard_map/pallas_call | solution.py:687

commit v5 on v4

--- a/solution.py
+++ b/solution.py
@@ -78,23 +78,55 @@
 
 class Sems:
     def __init__(self, send, recv):
-        self.send, self.recv, self.used = send, recv, 0
+        self.send, self.recv = send, recv
+        self.sends, self.recvs, self.shared = 0, 0, {}
         self.sent = []
 
-    def copy(self, src, dst, device, only=None):
-        k = self.used
-        self.used += 1
-        copy = pltpu.make_async_remote_copy(
+    def slots(self, group, arrive):
+        if ("send", group) not in self.shared:
+            if group is not None:
+                self.shared["send", group] = self.sends
+            out = self.sends
+            self.sends += 1
+        else:
+            out = self.shared["send", group]
+        if not arrive:
+            into = self.recvs
+            self.recvs += 1
+        else:
+            into = self.shared.setdefault(("recv", group), self.recvs)
+            self.recvs = max(self.recvs, into + 1)
+        return self.send.at[out], self.recv.at[into]
+
+    def make(self, src, dst, device, group=None, arrive=False):
+        send, recv = self.slots(group, arrive)
+        return pltpu.make_async_remote_copy(
             src_ref=src,
             dst_ref=dst,
-            send_sem=self.send.at[k],
-            recv_sem=self.recv.at[k],
+            send_sem=send,
+            recv_sem=recv,
             device_id=device,
             device_id_type=MESH,
         )
+
+    def copy(self, src, dst, device, only=None, group=None, arrive=False):
+        copy = self.make(src, dst, device, group, arrive)
         when(only, copy.start)
-        self.sent.append((only, copy))
+        if group is None:
+            self.sent.append((only, copy))
         return copy
+
+    def whole(self, ref, device, group):
+        send = self.send.at[self.shared["send", group]]
+        recv = self.recv.at[self.shared.get(("recv", group), 0)]
+        return pltpu.make_async_remote_copy(
+            src_ref=ref,
+            dst_ref=ref,
+            send_sem=send,
+            recv_sem=recv,
+            device_id=device,
+            device_id_type=MESH,
+        )
 
 
 def kernel(
@@ -187,28 +219,30 @@
         piece = quarter(head, xor(seq, mask))
         source = piece if mask else lat_ref.at[at(head, sub, sub)]
         for to in [1] if mask else zmoves + [1]:
-            by_seq[mask | to] = sems.copy(source, piece, on_seq(xor(seq, to)))
+            by_seq[mask | to] = sems.copy(
+                source, piece, on_seq(xor(seq, to)), group="lat"
+            )
 
     def relay(mask):
         by_seq[mask].wait_recv()
         if not mask & 1:
             forward(mask)
         piece = quarter(head, xor(seq, mask))
-        by_y[mask] = sems.copy(piece, piece, across)
-        by_core[mask] = sems.copy(piece, piece, other)
+        by_y[mask] = sems.copy(piece, piece, across, group="lat")
+        by_core[mask] = sems.copy(piece, piece, other, group="lat")
 
     def relay_y(mask):
         by_y[mask].wait_recv()
         piece = quarter(flip(head, 1), xor(seq, mask))
-        by_both[mask] = sems.copy(piece, piece, other)
+        by_both[mask] = sems.copy(piece, piece, other, group="lat")
 
     loads[0].wait()
     pl.semaphore_wait(barrier, nseq + heads + (core - x) * (core - x))
     forward(0)
     loads[3].wait()
-    pos_got = [
-        sems.copy(pos_ref, pos.at[seq], on_seq(xor(seq, mask))) for mask in range(1, nseq)
-    ]
+    for mask in range(1, nseq):
+        sems.copy(pos_ref, pos.at[seq], on_seq(xor(seq, mask)), group="pos", arrive=True)
+    pos_got = sems.whole(pos.at[pl.ds(0, nseq - 1)], other, "pos")
     for copy in loads[1:3]:
         copy.wait()
     for h in range(heads):
@@ -282,25 +316,27 @@
     keys_of(seq)
     for mask in zmoves:
         relay(mask | 1)
-    for mask in zmoves + [1]:
+    pos_got.wait_recv()
+    early = range(heads // 2)
+    for k in early:
+        turn(k)
+    steps = zmoves + [1] + [mask | 1 for mask in zmoves]
+    behind = [0]
+    for mask in steps:
         relay_y(mask)
-    for copy in pos_got:
-        copy.wait_recv()
-    for k in range(heads // 2):
-        turn(k)
-    for mask in zmoves + [1]:
-        block_of(mask)
-    for mask in zmoves:
-        relay_y(mask | 1)
-    early = [0] + zmoves + [1]
-    for mask in early:
-        for k in range(heads // 2):
-            scores_of(xor(seq, mask), k)
-    for mask in zmoves:
-        block_of(mask | 1)
-    for mask in zmoves:
-        for k in range(heads // 2):
-            scores_of(xor(seq, mask | 1), k)
+        if len(behind) > 2:
+            block = behind.pop(1)
+            block_of(block)
+            for k in early:
+                scores_of(xor(seq, block), k)
+        elif behind == [0]:
+            for k in early:
+                scores_of(seq, k)
+        behind.append(mask)
+    for block in behind[1:]:
+        block_of(block)
+        for k in early:
+            scores_of(xor(seq, block), k)
     for k in range(heads // 2, heads):
         turn(k)
         for mask in [0] + masks:
@@ -413,7 +449,11 @@
         piece_at = fin.at[a, r, c]
         for b in bits:
             moved[a, i, mask | (1 << b)] = sems.copy(
-                piece_at if mask else source(a, i, w), piece_at, on_seq(flip(seq, b)), active
+                piece_at if mask else source(a, i, w),
+                piece_at,
+                on_seq(flip(seq, b)),
+                active,
+                "z" if b else "x",
             )
 
     def spread_z(a, i, mask):
@@ -454,6 +494,21 @@
         sum_end(0, i)
         spread_z(0, i, 0)
         spread_x(0, i, 0)
+    dqt[...] = nt(kt[...], ds[...]).astype(BF16)
+    dq_in = [
+        sems.copy(
+            dqt.at[:, at(pick(xor(seq, 2 * k), slot_bits), rows, rows)],
+            dqr.at[u],
+            swap(k),
+            None if k else passive,
+        )
+        for k in range(heads)
+    ]
+
+    @pl.when(active)
+    def _():
+        dqr[u] = dqt[:, at(u, rows, rows)]
+
     def keys_grad(k, carry):
         here = at(k, tile, tile)
         got = nn(qd[:D_QK, :], ds[:, here]).astype(BF16)
@@ -474,14 +529,14 @@
         for h in range(nhead):
             lg[h, k] = got[h * sub : (h + 1) * sub]
         to_core[k] = [
-            sems.copy(lg.at[t * 2 + 1 - core, k], rc.at[j, k], other)
+            sems.copy(lg.at[t * 2 + 1 - core, k], rc.at[j, k], other, group="wide")
             for j, t in ((0, 1 - y), (1, y))
         ]
 
     def add_core(k):
         to_core[k][0].wait_recv()
         lg[others, k] = (lg[others, k].astype(F32) + rc[0, k].astype(F32)).astype(BF16)
-        to_y[k] = sems.copy(lg.at[others, k], ry.at[k], across)
+        to_y[k] = sems.copy(lg.at[others, k], ry.at[k], across, group="wide")
         to_core[k][1].wait_recv()
         lg[mine, k] = (lg[mine, k].astype(F32) + rc[1, k].astype(F32)).astype(BF16)
 
@@ -489,7 +544,10 @@
         to_y[k].wait_recv()
         lg[mine, k] = (lg[mine, k].astype(F32) + ry[k].astype(F32)).astype(BF16)
         to_x[k] = sems.copy(
-            lg.at[mine, k, :, at(1 - x, rows, rows)], rx.at[k], on_seq(flip(seq, 0))
+            lg.at[mine, k, :, at(1 - x, rows, rows)],
+            rx.at[k],
+            on_seq(flip(seq, 0)),
+            group="narrow",
         )
 
     def add_x(k):
@@ -497,7 +555,7 @@
         kept = lg[mine, k, :, at(x, rows, rows)].astype(F32) + rx[k].astype(F32)
         ac[k] = kept.astype(BF16)
         if k:
-            to_z[k] = sems.copy(ac.at[k], rz.at[k], on_seq(xor(seq, 2 * k)))
+            to_z[k] = sems.copy(ac.at[k], rz.at[k], on_seq(xor(seq, 2 * k)), group="narrow")
 
     chunks = [(a, i) for a in range(2) for i in range(subs)]
     values, keys = chunks[:subs], chunks[subs:]
@@ -530,10 +588,11 @@
                 spread_x(*chunk, mask)
             finish(*chunk, mask)
 
-    dqt[...] = nt(kt[...], ds[...]).astype(BF16)
     for mask in near_z[1:][::-1]:
         along_z(values, mask)
     drain(first_sent)
+    sems.whole(lat.at[:, pl.ds(0, (nseq - 1) * rows)], other, "lat").wait_send()
+    pos_got.wait_send()
     for k in zmasks[:-3]:
         add_y(k)
     for mask in near_z[1:][::-1]:
@@ -550,20 +609,6 @@
         add_y(k)
     for move in held:
         spread_x(*move)
-    dq_in = [
-        sems.copy(
-            dqt.at[:, at(pick(xor(seq, 2 * k), slot_bits), rows, rows)],
-            dqr.at[u],
-            swap(k),
-            None if k else passive,
-        )
-        for k in range(heads)
-    ]
-
-    @pl.when(active)
-    def _():
-        dqr[u] = dqt[:, at(u, rows, rows)]
-
     for k in zmasks[1:-1]:
         add_x(k)
     last_sent, sems.sent = sems.sent, []
@@ -575,16 +620,18 @@
         to_z[k].wait_recv()
         total = total + rz[k].astype(F32)
     fl[head] = total.astype(BF16)
-    first = sems.copy(fl.at[head], fl.at[head], across)
-    second = sems.copy(fl.at[head], fl.at[head], other)
+    first = sems.copy(fl.at[head], fl.at[head], across, group="narrow")
+    second = sems.copy(fl.at[head], fl.at[head], other, group="narrow")
     drain(last_sent)
+    when(active, sems.whole(fin.at[:, : D_LAT * (nz - 1) // nz], other, "z").wait_send)
+    sems.whole(lg.at[: nhead - 1], other, "wide").wait_send()
     for copy in dq_in[1:]:
         copy.wait_recv()
     when(passive, dq_in[0].wait_recv)
     for h in range(heads):
         dq_ref[:, h * D_QK : (h + 1) * D_QK] = dqr[h].T
     first.wait_recv()
-    third = sems.copy(fl.at[others], fl.at[others], other)
+    third = sems.copy(fl.at[others], fl.at[others], other, group="narrow")
     for mask in [0] + zmoves:
         for chunk in chunks:
             arrive(*chunk, mask | 1)
@@ -593,7 +640,10 @@
     third.wait_recv()
     for h in range(nhead):
         dl_ref[h * sub : (h + 1) * sub, :] = fl[h].astype(F32)
+    assert (sems.sends, sems.recvs) == (send.shape[0], recv.shape[0])
     drain(sems.sent)
+    when(active, sems.whole(fin, other, "x").wait_send)
+    sems.whole(lat.at[: 2 * sub, pl.ds(0, (nz + 1) * rows)], other, "narrow").wait_send()
 
 
 def store(*refs):
@@ -614,8 +664,10 @@
         share = D_LAT // groups
         sub = D_ALL // nhead
         cols = key_up.shape[1]
-        copies = (nseq - 1) * 5 + 2 * heads + 1
-        copies += 2 * subs * (2 * groups - 1 + nseq - 1) + 5 * nz + 3
+        sums = 2 * subs * (2 * groups - 1)
+        sends = 2 * heads + 1 + sums + 6
+        copies = (nseq - 1) * 4 + 1 + 2 * heads + 1
+        copies += sums + 2 * subs * (nseq - 1) + 5 * nz + 2
         vmem = pl.BlockSpec(memory_space=pltpu.VMEM)
         body = lambda *refs: kernel(nseq, nhead, subs, *refs)
         moved = [
@@ -675,7 +727,7 @@
             scratch_shapes=[pltpu.VMEM(shape, dtype) for shape, dtype in moved]
             + [pltpu.SemaphoreType.DMA((6,))]
             + [pltpu.VMEM(shape, dtype) for shape, dtype in scratch]
-            + [pltpu.SemaphoreType.DMA((copies,)), pltpu.SemaphoreType.DMA((copies,))],
+            + [pltpu.SemaphoreType.DMA((sends,)), pltpu.SemaphoreType.DMA((copies,))],
             compiler_params=pltpu.CompilerParams(
                 collective_id=0, has_side_effects=True, vmem_limit_bytes=min(limit, 60 * 1024 * 1024)
             ),

time: 49.9 us -> 48.3 us (0.968)
  Pallas kernels: 48.7 us -> 47.5 us
    pallas_call x1, Pallas kernels: 47.2 us -> 46 us  [shards(): pl.pallas_call(body, out_shape=(jax.ShapeDtypeStruct(queries.shape, BF16)...]
where the time goes in v5:
time: 48.3 us; the launch traced here: 48.1 us
  Pallas kernels  47.5 us (98%)
  between operations  0.64 us (1%)
    pallas_call x1, Pallas kernels, shards(): pl.pallas_call(body, out_shape=(jax.ShapeDtypeStruct(queries.shape, BF16)...  46 us
    pallas_call x1, Pallas kernels, shards(): pl.pallas_call(store, out_shape=[jax.ShapeDtypeStruct(a.shape, a.dtype) f...  1.51 us

profile of v5, /device:TPU:0, one launch (start us, length us, event | category | flops | bytes accessed | tf_op | source)
XLA Modules:
  0.0 48.1 jit_solution(13406011391352391813)
XLA Ops:
  0.6 46.0 %shard_map.93 = (bf16[128,768]{1,0:T(8,128)(2,1)S(1)}, f32[576,128]{1,0:T(8,128)S(1)}, f32[512,512]{1,0:T(8,128)S(1)}, f32[512,512]{1,0:T(8,128)S(1)}) custom-call(bf16[128,768]{1,0:T(8,128)(2,1)} %refs_0_.1, bf16[576,128]{1,0:T(8,128)(2,1)} %bitcast.3, bf16[512,512]{1,0:T(8,128)(2,1)} %refs_2_.1, bf16[512,512]{1,0:T(8,128)(2,1)} %refs_3_.1, ...), custom_call_target="tpu_custom_call" | custom-call | tf_op jit(solution)/shard_map/pallas_call | solution.py:717
  46.6 1.5 %shard_map.94 = (bf16[128,768]{1,0:T(8,128)(2,1)}, f32[576,128]{1,0:T(8,128)}, f32[512,512]{1,0:T(8,128)}, f32[512,512]{1,0:T(8,128)}) custom-call(bf16[128,768]{1,0:T(8,128)(2,1)S(1)} %get-tuple-element.12.refs_0_, f32[576,128]{1,0:T(8,128)S(1)} %get-tuple-element.13.refs_1_, f32[512,512]{1,0:T(8,128)S(1)} %get-tuple-element.14.refs_2_, ...), custom_call_target="tpu_custom_call" | custom-call | tf_op jit(solution)/shard_map/pallas_call | solution.py:739

commit v6 on v5

--- a/solution.py
+++ b/solution.py
@@ -295,6 +295,24 @@
                 top = jnp.maximum(top, got[:, c * LANE : (c + 1) * LANE])
             mx[part, :] = top
 
+    def scores_pair(p, k):
+        here = slice(2 * p * rows, 2 * (p + 1) * rows)
+        keys, vals = kt[:, here], vt[:, here]
+        rel = jnp.concatenate([pos[2 * p] - down, pos[2 * p + 1] - down], axis=1)
+        first = pos[xor(seq, 2 * k) + core - x] - lane
+        slot = pick(xor(seq, 2 * k), slot_bits)
+        for t in range(per):
+            part = at(slot * per + t, STRIPE, STRIPE)
+            base = first[:, t * STRIPE : (t + 1) * STRIPE]
+            base = jnp.concatenate([base] * (2 * per), axis=1)
+            got = jnp.where(rel <= base, nn(qall[part, :], keys), NEG)
+            sc[part, here] = got
+            dp[part, here] = nn(dall[part, :], vals)
+            top = mx[part, :]
+            for c in range(2 * rows // LANE):
+                top = jnp.maximum(top, got[:, c * LANE : (c + 1) * LANE])
+            mx[part, :] = top
+
     def turn(k):
         if k:
             q_got[k].wait_recv()
@@ -314,12 +332,13 @@
     when(passive, kuv_got.wait_recv)
     ut[...] = kuv[...].T
     keys_of(seq)
-    for mask in zmoves:
+    early = range(heads // 2)
+    relay(zmoves[0] | 1)
+    turn(0)
+    for mask in zmoves[1:]:
         relay(mask | 1)
     pos_got.wait_recv()
-    early = range(heads // 2)
-    for k in early:
-        turn(k)
+    turn(1)
     steps = zmoves + [1] + [mask | 1 for mask in zmoves]
     behind = [0]
     for mask in steps:
@@ -339,8 +358,8 @@
             scores_of(xor(seq, block), k)
     for k in range(heads // 2, heads):
         turn(k)
-        for mask in [0] + masks:
-            scores_of(xor(seq, mask), k)
+        for p in range(nz):
+            scores_pair(p, k)
 
     first_sent, sems.sent = sems.sent, []
 
@@ -528,6 +547,8 @@
         got = jnp.concatenate([got, rp[:, here]], axis=0)
         for h in range(nhead):
             lg[h, k] = got[h * sub : (h + 1) * sub]
+
+    def share_fold(k):
         to_core[k] = [
             sems.copy(lg.at[t * 2 + 1 - core, k], rc.at[j, k], other, group="wide")
             for j, t in ((0, 1 - y), (1, y))
@@ -564,6 +585,8 @@
 
     for k in zmasks:
         fold(k)
+    for k in zmasks:
+        share_fold(k)
     up[1] = nt(lat[:D_LAT, :], kvg[:D_NOPE, :]).astype(BF16)
     for i in range(subs):
         sum_start(1, i)
@@ -593,24 +616,22 @@
     drain(first_sent)
     sems.whole(lat.at[:, pl.ds(0, (nseq - 1) * rows)], other, "lat").wait_send()
     pos_got.wait_send()
-    for k in zmasks[:-3]:
+    for k in zmasks[:-1]:
         add_y(k)
     for mask in near_z[1:][::-1]:
         along_z(keys, mask)
-    for k in zmasks[-3:-2]:
-        add_y(k)
+    for k in zmasks[:-3]:
+        add_x(k)
     along_z(values, near_z[0])
-    for k in zmasks[-2:-1]:
-        add_y(k)
-    along_z(keys, near_z[0], True)
-    for k in zmasks[:1]:
-        add_x(k)
     for k in zmasks[-1:]:
         add_y(k)
+    for k in zmasks[-3:-2]:
+        add_x(k)
+    along_z(keys, near_z[0], True)
+    for k in zmasks[-2:-1]:
+        add_x(k)
     for move in held:
         spread_x(*move)
-    for k in zmasks[1:-1]:
-        add_x(k)
     last_sent, sems.sent = sems.sent, []
     for mask in far_z:
         along_z(chunks, mask)

time: 48.3 us -> 47.4 us (0.981)
  Pallas kernels: 47.5 us -> 46.6 us
    pallas_call x1, Pallas kernels: 46 us -> 45.1 us  [shards(): pl.pallas_call(body, out_shape=(jax.ShapeDtypeStruct(queries.shape, BF16)...]
where the time goes in v6:
time: 47.4 us; the launch traced here: 47.3 us
  Pallas kernels  46.6 us (98%)
  between operations  0.64 us (1%)
    pallas_call x1, Pallas kernels, shards(): pl.pallas_call(body, out_shape=(jax.ShapeDtypeStruct(queries.shape, BF16)...  45.1 us
    pallas_call x1, Pallas kernels, shards(): pl.pallas_call(store, out_shape=[jax.ShapeDtypeStruct(a.shape, a.dtype) f...  1.51 us

profile of v6, /device:TPU:0, one launch (start us, length us, event | category | flops | bytes accessed | tf_op | source)
XLA Modules:
  0.0 47.3 jit_solution(5712325814577246995)
XLA Ops:
  0.6 45.1 %shard_map.93 = (bf16[128,768]{1,0:T(8,128)(2,1)S(1)}, f32[576,128]{1,0:T(8,128)S(1)}, f32[512,512]{1,0:T(8,128)S(1)}, f32[512,512]{1,0:T(8,128)S(1)}) custom-call(bf16[128,768]{1,0:T(8,128)(2,1)} %refs_0_.1, bf16[576,128]{1,0:T(8,128)(2,1)} %bitcast.3, bf16[512,512]{1,0:T(8,128)(2,1)} %refs_2_.1, bf16[512,512]{1,0:T(8,128)(2,1)} %refs_3_.1, ...), custom_call_target="tpu_custom_call" | custom-call | tf_op jit(solution)/shard_map/pallas_call | solution.py:738
  45.7 1.5 %shard_map.94 = (bf16[128,768]{1,0:T(8,128)(2,1)}, f32[576,128]{1,0:T(8,128)}, f32[512,512]{1,0:T(8,128)}, f32[512,512]{1,0:T(8,128)}) custom-call(bf16[128,768]{1,0:T(8,128)(2,1)S(1)} %get-tuple-element.12.refs_0_, f32[576,128]{1,0:T(8,128)S(1)} %get-tuple-element.13.refs_1_, f32[512,512]{1,0:T(8,128)S(1)} %get-tuple-element.14.refs_2_, ...), custom_call_target="tpu_custom_call" | custom-call | tf_op jit(solution)/shard_map/pallas_call | solution.py:760

commit v7 on v6

--- a/solution.py
+++ b/solution.py
@@ -163,11 +163,12 @@
 
     other = on_head(flip(head, 0))
     across = on_head(flip(head, 1))
+    corner = on_head(flip(flip(head, 0), 1))
 
     barrier = pltpu.get_barrier_semaphore()
     for mask in range(1, nseq):
         pl.semaphore_signal(barrier, inc=1, device_id=on_seq(xor(seq, mask)), device_id_type=MESH)
-    for device in (other, across):
+    for device in (other, across, corner):
         pl.semaphore_signal(barrier, inc=1, device_id=device, device_id_type=MESH)
 
     def swap(k):
@@ -237,7 +238,7 @@
         by_both[mask] = sems.copy(piece, piece, other, group="lat")
 
     loads[0].wait()
-    pl.semaphore_wait(barrier, nseq + heads + (core - x) * (core - x))
+    pl.semaphore_wait(barrier, nseq + heads + 1 + (core - x) * (core - x))
     forward(0)
     loads[3].wait()
     for mask in range(1, nseq):
@@ -642,6 +643,7 @@
         total = total + rz[k].astype(F32)
     fl[head] = total.astype(BF16)
     first = sems.copy(fl.at[head], fl.at[head], across, group="narrow")
+    third = sems.copy(fl.at[head], fl.at[head], corner, group="narrow")
     second = sems.copy(fl.at[head], fl.at[head], other, group="narrow")
     drain(last_sent)
     when(active, sems.whole(fin.at[:, : D_LAT * (nz - 1) // nz], other, "z").wait_send)
@@ -652,7 +654,6 @@
     for h in range(heads):
         dq_ref[:, h * D_QK : (h + 1) * D_QK] = dqr[h].T
     first.wait_recv()
-    third = sems.copy(fl.at[others], fl.at[others], other, group="narrow")
     for mask in [0] + zmoves:
         for chunk in chunks:
             arrive(*chunk, mask | 1)

time: 47.4 us -> 46.7 us (0.985)
  Pallas kernels: 46.6 us -> 45.9 us
    pallas_call x1, Pallas kernels: 45.1 us -> 44.4 us  [shards(): pl.pallas_call(body, out_shape=(jax.ShapeDtypeStruct(queries.shape, BF16)...]
where the time goes in v7:
time: 46.7 us; the launch traced here: 46.5 us
  Pallas kernels  45.9 us (98%)
  between operations  0.64 us (1%)
    pallas_call x1, Pallas kernels, shards(): pl.pallas_call(body, out_shape=(jax.ShapeDtypeStruct(queries.shape, BF16)...  44.4 us
    pallas_call x1, Pallas kernels, shards(): pl.pallas_call(store, out_shape=[jax.ShapeDtypeStruct(a.shape, a.dtype) f...  1.51 us

profile of v7, /device:TPU:0, one launch (start us, length us, event | category | flops | bytes accessed | tf_op | source)
XLA Modules:
  0.0 46.5 jit_solution(1639801888143417252)
XLA Ops:
  0.6 44.4 %shard_map.93 = (bf16[128,768]{1,0:T(8,128)(2,1)S(1)}, f32[576,128]{1,0:T(8,128)S(1)}, f32[512,512]{1,0:T(8,128)S(1)}, f32[512,512]{1,0:T(8,128)S(1)}) custom-call(bf16[128,768]{1,0:T(8,128)(2,1)} %refs_0_.1, bf16[576,128]{1,0:T(8,128)(2,1)} %bitcast.3, bf16[512,512]{1,0:T(8,128)(2,1)} %refs_2_.1, bf16[512,512]{1,0:T(8,128)(2,1)} %refs_3_.1, ...), custom_call_target="tpu_custom_call" | custom-call | tf_op jit(solution)/shard_map/pallas_call | solution.py:739
  45.0 1.5 %shard_map.94 = (bf16[128,768]{1,0:T(8,128)(2,1)}, f32[576,128]{1,0:T(8,128)}, f32[512,512]{1,0:T(8,128)}, f32[512,512]{1,0:T(8,128)}) custom-call(bf16[128,768]{1,0:T(8,128)(2,1)S(1)} %get-tuple-element.12.refs_0_, f32[576,128]{1,0:T(8,128)S(1)} %get-tuple-element.13.refs_1_, f32[512,512]{1,0:T(8,128)S(1)} %get-tuple-element.14.refs_2_, ...), custom_call_target="tpu_custom_call" | custom-call | tf_op jit(solution)/shard_map/pallas_call | solution.py:761
